TPU v7x, 32 devices: a whole 2x2x4 slice. The times are simulated.
32 devices in a mesh: ctx: 8 (over y, x, core), fsdp: 4 (over z).
Axes of the slice: x: 2, y: 2, z: 4, core: 2. Of those that a mesh axis runs over, the one named last changes fastest.
Arguments:
- tokens: bfloat16 [4, 1024, 2048], P('fsdp', 'ctx'), may hold values from -70 to 70
- block_order: int32 [4, 16], P('fsdp'), may hold values from 0 to 15, each once within a row
- w_query: bfloat16 [2048, 2048], P('fsdp')
- w_key: bfloat16 [2048, 2048], P('fsdp'), may hold values from -2 to 2
- w_value: bfloat16 [2048, 2048], P('fsdp'), may hold values from -0.125 to 0.125
- w_out: bfloat16 [2048, 2048], P('fsdp'), may hold values from -2 to 2
- w_gate: bfloat16 [2048, 8192], P('fsdp'), may hold values from -0.125 to 0.125
- w_up: bfloat16 [2048, 8192], P('fsdp'), may hold values from -0.125 to 0.125
- w_down: bfloat16 [2048, 8192], P('fsdp'), may hold values from -0.0625 to 0.0625
- norm_attn: bfloat16 [2048], P('fsdp'), may hold values from 0.5 to 1.5
- norm_mlp: bfloat16 [2048], P('fsdp'), may hold values from 0.5 to 1.5
- cotangent: bfloat16 [4, 1024, 2048], P('fsdp', 'ctx'), may hold values from -6 to 6
Outputs:
- output: float32 [4, 1024, 2048], P('fsdp', 'ctx')
- grad_tokens: float32 [4, 1024, 2048], P('fsdp', 'ctx')
- grad_query: float32 [2048, 2048], P('fsdp', 'ctx')
- grad_key: float32 [2048, 2048], P('fsdp', 'ctx')
- grad_value: float32 [2048, 2048], P('fsdp', 'ctx')
- grad_out: float32 [2048, 2048], P('fsdp', 'ctx')
- grad_gate: float32 [2048, 8192], P('fsdp', 'ctx')
- grad_up: float32 [2048, 8192], P('fsdp', 'ctx')
- grad_down: float32 [2048, 8192], P('fsdp', 'ctx')
- grad_norm_attn: float32 [2048], P('fsdp')
- grad_norm_mlp: float32 [2048], P('fsdp')
Inputs may be any that keep to these rules, and one draw needn't show every extreme that they name: `block_order`: each row lists each of the 16 blocks of its sequence once.
All inputs are finite; a program needn't handle non-finite values.
Results may differ from a plain program's by a relative error of at most 0.018.
Values may be sent and summed in bfloat16 or wider, within the bound.
A program may use at most 448 MiB of HBM per device.

v0:
```python
import jax
import jax.numpy as jnp
from jax import lax
from jax.sharding import PartitionSpec as P

HEADS = 32
HD = 64


eps = 1e-05
rope_base = 130000.0
neg_large = -1e30


def passed_along(block, axis, distance):
    devices = range(lax.axis_size(axis))
    route = [((i - distance) % len(devices), i) for i in devices]
    return lax.ppermute(block, axis, route)


def rms_scale(values):
    return lax.rsqrt(jnp.mean(values * values, axis=-1, keepdims=True) + eps)


def norm_back(grad_normed, normed, scaling):
    return scaling * (grad_normed - normed * jnp.mean(grad_normed * normed, axis=-1, keepdims=True))


def slot_positions(layout, row_ids, half_rows):
    slots = row_ids // half_rows
    onehot = slots[:, None] == jnp.arange(layout.shape[0], dtype=jnp.int32)[None, :]
    return jnp.sum(jnp.where(onehot, layout[None, :], 0), axis=1) * half_rows + row_ids % half_rows


def rotation_tables(positions, head_size):
    half_size = head_size // 2
    freqs = rope_base ** (-(jnp.arange(half_size, dtype=jnp.float32) * (2.0 / head_size)))
    angles = positions.astype(jnp.float32)[:, None] * freqs[None, :]
    cosine = jnp.concatenate([jnp.cos(angles), jnp.cos(angles)], axis=-1)[:, None, :]
    sine = jnp.concatenate([jnp.sin(angles), jnp.sin(angles)], axis=-1)[:, None, :]
    return (cosine, sine)


def rotate(values, cosine, sine):
    half_size = values.shape[-1] // 2
    turned = jnp.concatenate([-values[..., half_size:], values[..., :half_size]], axis=-1)
    return values * cosine + turned * sine


def rotate_back(grads, cosine, sine):
    half_size = grads.shape[-1] // 2
    scaled = grads * sine
    turned = jnp.concatenate([scaled[..., half_size:], -scaled[..., :half_size]], axis=-1)
    return grads * cosine + turned


def contract_last(left, right):
    return lax.dot_general(
        left, right, (((1,), (1,)), ((), ())), preferred_element_type=jnp.float32
    )


def online_step(carried, key_block, query_rot, query_pos, scaling):
    maxima, totals, accum = carried
    keys_now, values_now, key_pos = key_block
    scores = (
        jnp.einsum("qhd,khd->hqk", query_rot, keys_now, preferred_element_type=jnp.float32)
        * scaling
    )
    allowed = (key_pos[None, :] <= query_pos[:, None])[None]
    new_max = jnp.maximum(maxima, jnp.max(jnp.where(allowed, scores, neg_large), axis=-1))
    factor = jnp.exp(maxima - new_max)
    probs = jnp.where(allowed, jnp.exp(scores - new_max[..., None]), 0.0)
    totals = totals * factor + jnp.sum(probs, axis=-1)
    accum = accum * factor.T[:, :, None] + jnp.einsum(
        "hqk,khd->qhd", probs.astype(jnp.bfloat16), values_now, preferred_element_type=jnp.float32
    )
    return (new_max, totals, accum)


def back_step(
    keys_now, values_now, key_pos, query_rot, query_pos, grad_attn_heads, log_totals, delta, scaling
):
    scores = (
        jnp.einsum("qhd,khd->hqk", query_rot, keys_now, preferred_element_type=jnp.float32)
        * scaling
    )
    allowed = (key_pos[None, :] <= query_pos[:, None])[None]
    probs = jnp.where(allowed, jnp.exp(scores - log_totals[..., None]), 0.0)
    part_v = jnp.einsum(
        "hqk,qhd->khd",
        probs.astype(jnp.bfloat16),
        grad_attn_heads,
        preferred_element_type=jnp.float32,
    )
    grad_probs = jnp.einsum(
        "qhd,khd->hqk", grad_attn_heads, values_now, preferred_element_type=jnp.float32
    )
    grad_scores = (probs * (grad_probs - delta[..., None]) * scaling).astype(jnp.bfloat16)
    part_q = jnp.einsum("hqk,khd->qhd", grad_scores, keys_now, preferred_element_type=jnp.float32)
    part_k = jnp.einsum("hqk,qhd->khd", grad_scores, query_rot, preferred_element_type=jnp.float32)
    return (part_q, part_k, part_v)


def send_grads(grad_keys, grad_values):
    return (
        passed_along(grad_keys.astype(jnp.bfloat16), "ctx", 1).astype(grad_keys.dtype),
        passed_along(grad_values.astype(jnp.bfloat16), "ctx", 1).astype(grad_values.dtype),
    )


def on_device(
    tokens,
    block_order,
    w_query,
    w_key,
    w_value,
    w_out,
    w_gate,
    w_up,
    w_down,
    norm_attn,
    norm_mlp,
    cotangent,
):
    inputs = tokens[0].astype(jnp.float32)
    tok_rows = inputs.shape[0]
    model_width = inputs.shape[1]
    head_count = HEADS
    head_size = HD
    scaling = head_size ** (-0.5)
    half_rows = tok_rows // 2
    layout = block_order[0]
    ctx_size = lax.axis_size("ctx")
    ctx_place = lax.axis_index("ctx")
    fsdp_size = lax.axis_size("fsdp")
    fsdp_place = lax.axis_index("fsdp")
    local_rows = jnp.arange(tok_rows, dtype=jnp.int32)
    query_pos = slot_positions(layout, ctx_place * tok_rows + local_rows, half_rows)
    cosine, sine = rotation_tables(query_pos, head_size)
    zeros_model = jnp.zeros((tok_rows, model_width), jnp.float32)
    zeros_heads = jnp.zeros((tok_rows, head_count, head_size), jnp.float32)
    scale_attn = rms_scale(inputs)
    normed_attn = inputs * scale_attn
    piece_query = lax.all_gather(w_query, "fsdp", axis=0, tiled=True)
    piece_key = lax.all_gather(w_key, "fsdp", axis=0, tiled=True)
    piece_value = lax.all_gather(w_value, "fsdp", axis=0, tiled=True)
    piece_gain = lax.all_gather(norm_attn, "fsdp", axis=0, tiled=True)
    normed_part = normed_attn
    hidden_part = (normed_part * piece_gain.astype(jnp.float32)[None, :]).astype(jnp.bfloat16)
    query = jnp.dot(hidden_part, piece_query, preferred_element_type=jnp.float32)
    keyed = jnp.dot(hidden_part, piece_key, preferred_element_type=jnp.float32)
    valued = jnp.dot(hidden_part, piece_value, preferred_element_type=jnp.float32)
    hidden_attn = hidden_part
    query_rot = rotate(query.reshape(tok_rows, head_count, head_size), cosine, sine).astype(
        jnp.bfloat16
    )
    key_rot = rotate(keyed.reshape(tok_rows, head_count, head_size), cosine, sine).astype(
        jnp.bfloat16
    )
    key_flat = key_rot.reshape(tok_rows, model_width)
    value_flat = valued.astype(jnp.bfloat16)
    start_state = (
        jnp.full((head_count, tok_rows), neg_large, jnp.float32),
        jnp.zeros((head_count, tok_rows), jnp.float32),
        zeros_heads,
    )
    carried = start_state
    key_piece = lax.all_gather(key_flat, "ctx", axis=0, tiled=True)
    value_piece = lax.all_gather(value_flat, "ctx", axis=0, tiled=True)
    piece_rows = key_piece.shape[0]
    block_count = piece_rows // tok_rows
    key_blocks = key_piece.reshape(block_count, tok_rows, head_count, head_size)
    value_blocks = value_piece.reshape(block_count, tok_rows, head_count, head_size)
    row_ids = jnp.arange(piece_rows, dtype=jnp.int32)
    key_pos = slot_positions(layout, row_ids, half_rows).reshape(block_count, tok_rows)

    def one_block(inner, key_block):
        return (online_step(inner, key_block, query_rot, query_pos, scaling), None)

    carried, unused_out = lax.scan(one_block, carried, (key_blocks, value_blocks, key_pos))
    maxima, totals, accum = carried
    log_totals = maxima + jnp.log(totals)
    attn_rows = (accum / totals.T[:, :, None]).reshape(tok_rows, model_width).astype(jnp.bfloat16)
    mid_stream = inputs + jnp.dot(
        attn_rows,
        lax.all_gather(w_out, "fsdp", axis=0, tiled=True),
        preferred_element_type=jnp.float32,
    )
    scale_mlp = rms_scale(mid_stream)
    normed_mlp = mid_stream * scale_mlp
    piece_gate = lax.all_gather(w_gate, "fsdp", axis=0, tiled=True)
    piece_up = lax.all_gather(w_up, "fsdp", axis=0, tiled=True)
    piece_gain = lax.all_gather(norm_mlp, "fsdp", axis=0, tiled=True)
    normed_part = normed_mlp
    hidden_part = (normed_part * piece_gain.astype(jnp.float32)[None, :]).astype(jnp.bfloat16)
    gate_pre = jnp.dot(hidden_part, piece_gate, preferred_element_type=jnp.float32)
    up_pre = jnp.dot(hidden_part, piece_up, preferred_element_type=jnp.float32)
    sigmoid_gate = jax.nn.sigmoid(gate_pre)
    silu_gate = gate_pre * sigmoid_gate
    acted = (silu_gate * up_pre).astype(jnp.bfloat16)
    result = mid_stream + contract_last(acted, lax.all_gather(w_down, "fsdp", axis=0, tiled=True))
    grad_b = cotangent[0]
    grad_act = jnp.dot(
        grad_b,
        lax.all_gather(w_down, "fsdp", axis=0, tiled=True),
        preferred_element_type=jnp.float32,
    )
    grad_gate_pre = (
        grad_act * up_pre * sigmoid_gate * (1.0 + gate_pre * (1.0 - sigmoid_gate))
    ).astype(jnp.bfloat16)
    grad_up_pre = (grad_act * silu_gate).astype(jnp.bfloat16)
    piece_gate = lax.all_gather(w_gate, "fsdp", axis=0, tiled=True)
    piece_up = lax.all_gather(w_up, "fsdp", axis=0, tiled=True)
    piece_gain = lax.all_gather(norm_mlp, "fsdp", axis=0, tiled=True)
    columns = contract_last(grad_gate_pre, piece_gate) + contract_last(grad_up_pre, piece_up)
    gain_mlp = piece_gain.astype(jnp.float32)
    gain_grad_mlp = jnp.sum(columns * normed_mlp, axis=0)
    grad_mid = grad_b.astype(jnp.float32) + norm_back(
        columns * gain_mlp[None, :], normed_mlp, scale_mlp
    )
    grad_mid_b = grad_mid.astype(jnp.bfloat16)
    whole_out, whole_query, whole_key, whole_value, gain_attn = (
        lax.all_gather(w_out, "fsdp", axis=0, tiled=True),
        lax.all_gather(w_query, "fsdp", axis=0, tiled=True),
        lax.all_gather(w_key, "fsdp", axis=0, tiled=True),
        lax.all_gather(w_value, "fsdp", axis=0, tiled=True),
        lax.all_gather(norm_attn, "fsdp", axis=0, tiled=True),
    )
    grad_attn = contract_last(grad_mid_b, whole_out).astype(jnp.bfloat16)
    grad_attn_heads = grad_attn.reshape(tok_rows, head_count, head_size)
    delta = jnp.sum(
        (grad_attn.astype(jnp.float32) * attn_rows.astype(jnp.float32)).reshape(
            tok_rows, head_count, head_size
        ),
        axis=-1,
    ).T

    def visit_core(turn_index, keys_now, values_now, grad_keys, grad_values, grad_query_acc):
        owner_index = (ctx_place - turn_index) % ctx_size
        key_pos = slot_positions(layout, owner_index * tok_rows + local_rows, half_rows)
        part_q, part_k, part_v = back_step(
            keys_now.reshape(tok_rows, head_count, head_size),
            values_now.reshape(tok_rows, head_count, head_size),
            key_pos,
            query_rot,
            query_pos,
            grad_attn_heads,
            log_totals,
            delta,
            scaling,
        )
        return (
            grad_keys + part_k.reshape(tok_rows, model_width),
            grad_values + part_v.reshape(tok_rows, model_width),
            grad_query_acc + part_q,
        )

    def visit(turn_index, carried):
        keys_now, values_now, grad_keys, grad_values, grad_query_acc = carried
        grad_keys, grad_values, grad_query_acc = visit_core(
            turn_index, keys_now, values_now, grad_keys, grad_values, grad_query_acc
        )
        keys_now, values_now = passed_along((keys_now, values_now), "ctx", 1)
        grad_keys, grad_values = send_grads(grad_keys, grad_values)
        return (keys_now, values_now, grad_keys, grad_values, grad_query_acc)

    keys_now, values_now, grad_keys, grad_values, grad_query_acc = lax.fori_loop(
        0, ctx_size - 1, visit, (key_flat, value_flat, zeros_model, zeros_model, zeros_heads)
    )
    grad_keys, grad_values, grad_query_acc = visit_core(
        ctx_size - 1, keys_now, values_now, grad_keys, grad_values, grad_query_acc
    )
    grad_keys, grad_values = send_grads(grad_keys, grad_values)
    grad_q = (
        rotate_back(grad_query_acc, cosine, sine)
        .reshape(tok_rows, model_width)
        .astype(jnp.bfloat16)
    )
    grad_k = (
        rotate_back(grad_keys.reshape(tok_rows, head_count, head_size), cosine, sine)
        .reshape(tok_rows, model_width)
        .astype(jnp.bfloat16)
    )
    grad_v = grad_values.astype(jnp.bfloat16)
    grad_hidden_attn = (
        contract_last(grad_q, whole_query)
        + contract_last(grad_k, whole_key)
        + contract_last(grad_v, whole_value)
    )
    gain_grad_attn = jnp.sum(grad_hidden_attn * normed_attn, axis=0)
    grad_input = grad_mid + norm_back(
        grad_hidden_attn * gain_attn.astype(jnp.float32)[None, :], normed_attn, scale_attn
    )
    row_share = model_width // fsdp_size
    left_factors = (hidden_attn, attn_rows, hidden_part, grad_b)
    right_factors = (grad_q, grad_k, grad_v, grad_mid_b, grad_gate_pre, grad_up_pre, acted)
    left_index = (0, 0, 0, 1, 2, 2, 3)
    outgoing = []
    for factor in left_factors:
        owned = factor.reshape(tok_rows, fsdp_size, row_share).transpose(1, 0, 2)
        spread = jnp.broadcast_to(owned[None], (ctx_size, fsdp_size, tok_rows, row_share))
        outgoing.append(spread.reshape(ctx_size * fsdp_size, tok_rows, row_share))
    for factor in right_factors:
        share = factor.shape[1] // ctx_size
        owned = factor.reshape(tok_rows, ctx_size, share).transpose(1, 0, 2)
        spread = jnp.broadcast_to(owned[:, None], (ctx_size, fsdp_size, tok_rows, share))
        outgoing.append(spread.reshape(ctx_size * fsdp_size, tok_rows, share))
    arrived = (
        lax.all_to_all(outgoing[0], ("ctx", "fsdp"), split_axis=0, concat_axis=0, tiled=True),
        lax.all_to_all(outgoing[1], ("ctx", "fsdp"), split_axis=0, concat_axis=0, tiled=True),
        lax.all_to_all(outgoing[2], ("ctx", "fsdp"), split_axis=0, concat_axis=0, tiled=True),
        lax.all_to_all(outgoing[3], ("ctx", "fsdp"), split_axis=0, concat_axis=0, tiled=True),
        lax.all_to_all(outgoing[4], ("ctx", "fsdp"), split_axis=0, concat_axis=0, tiled=True),
        lax.all_to_all(outgoing[5], ("ctx", "fsdp"), split_axis=0, concat_axis=0, tiled=True),
        lax.all_to_all(outgoing[6], ("ctx", "fsdp"), split_axis=0, concat_axis=0, tiled=True),
        lax.all_to_all(outgoing[7], ("ctx", "fsdp"), split_axis=0, concat_axis=0, tiled=True),
        lax.all_to_all(outgoing[8], ("ctx", "fsdp"), split_axis=0, concat_axis=0, tiled=True),
        lax.all_to_all(outgoing[9], ("ctx", "fsdp"), split_axis=0, concat_axis=0, tiled=True),
        lax.all_to_all(outgoing[10], ("ctx", "fsdp"), split_axis=0, concat_axis=0, tiled=True),
    )
    pieces_out = []
    for position in range(7):
        left_side = arrived[left_index[position]]
        right_side = arrived[4 + position]
        pieces_out.append(
            lax.dot_general(
                left_side,
                right_side,
                (((0, 1), (0, 1)), ((), ())),
                preferred_element_type=jnp.float32,
            )
        )
    gain_total = lax.psum(jnp.stack([gain_grad_attn, gain_grad_mlp]), ("ctx", "fsdp"))
    gain_own = lax.dynamic_slice_in_dim(gain_total, fsdp_place * row_share, row_share, 1)
    return (
        result[None],
        grad_input[None],
        pieces_out[0],
        pieces_out[1],
        pieces_out[2],
        pieces_out[3],
        pieces_out[4],
        pieces_out[5],
        pieces_out[6],
        gain_own[0],
        gain_own[1],
    )


def solution(mesh):
    in_specs = (
        P("fsdp", "ctx", None),
        P("fsdp", None),
        P("fsdp", None),
        P("fsdp", None),
        P("fsdp", None),
        P("fsdp", None),
        P("fsdp", None),
        P("fsdp", None),
        P("fsdp", None),
        P("fsdp"),
        P("fsdp"),
        P("fsdp", "ctx", None),
    )
    out_specs = (
        P("fsdp", "ctx", None),
        P("fsdp", "ctx", None),
        P("fsdp", "ctx"),
        P("fsdp", "ctx"),
        P("fsdp", "ctx"),
        P("fsdp", "ctx"),
        P("fsdp", "ctx"),
        P("fsdp", "ctx"),
        P("fsdp", "ctx"),
        P("fsdp"),
        P("fsdp"),
    )
    return jax.shard_map(
        on_device, mesh=mesh, in_specs=in_specs, out_specs=out_specs, check_vma=False
    )
```

profile of v0, /device:TPU:0, one launch (start us, length us, event | category | flops | bytes accessed | tf_op | source)
XLA Modules:
  0.0 3832.4 jit_solution(13162478585860778106)
XLA Ops:
  23.7 138.2 %all-gather.16.cloned.1.call-done = bf16[2048,2048]{1,0:T(8,128)(2,1)} async-done(((bf16[512,2048]{1,0:T(8,128)(2,1)}), bf16[2048,2048]{1,0:T(8,128)(2,1)}) %all-gather.16.cloned.1.call-update) | async-done | bytes 8388624 | tf_op jit(solution)/shard_map/all_gather | solution.py:145
  174.5 136.8 %all-gather.12.cloned.1.call-done = bf16[2048,2048]{1,0:T(8,128)(2,1)} async-done(((bf16[512,2048]{1,0:T(8,128)(2,1)}), bf16[2048,2048]{1,0:T(8,128)(2,1)}) %all-gather.12.cloned.1.call-update) | async-done | bytes 8388624 | tf_op jit(solution)/shard_map/all_gather | solution.py:146
  334.0 126.7 %all-gather.18.cloned.1.call-done = bf16[2048,2048]{1,0:T(8,128)(2,1)} async-done(((bf16[512,2048]{1,0:T(8,128)(2,1)}), bf16[2048,2048]{1,0:T(8,128)(2,1)}) %all-gather.18.cloned.1.call-update) | async-done | bytes 8388624 | tf_op jit(solution)/shard_map/all_gather | solution.py:147
  477.4 99.3 %all-gather.1 = bf16[4,1,512]{2,1,0:T(2,128)(2,1)S(1)} all-gather(bf16[1,1,512]{2,1,0:T(2,128)(2,1)S(1)} %reshape.514), channel_id=1, replica_groups=mesh['ctx'=8,'fsdp'=4] {'fsdp'}, dimensions={0}, use_global_device_ids=true | all-gather | bytes 5120 | tf_op jit(solution)/shard_map/all_gather | solution.py:194
  614.3 41.5 %while.40 = (s32[]{:T(128)}, f32[32,128]{1,0:T(8,128)S(1)}, f32[32,128]{1,0:T(8,128)S(1)}, f32[128,32,64]{0,2,1:T(8,128)}, s32[8,128]{1,0:T(8,128)S(1)}, /*index...) while((s32[]{:T(128)}, f32[32,128]{1,0:T(8,128)S(1)}, ...), condition=%wide.region_6.7_spmd.clone, body=%wide.region_3.6_spmd.clone.sunk | while | flops 140812288 | bytes 10292349 | solution.py:181
  657.2 160.8 %all-gather.22.cloned.1.call-done = bf16[2048,2048]{1,0:T(8,128)(2,1)} async-done(((bf16[512,2048]{1,0:T(8,128)(2,1)}), bf16[2048,2048]{1,0:T(8,128)(2,1)}) %all-gather.22.cloned.1.call-update) | async-done | bytes 8388624 | tf_op jit(solution)/shard_map/all_gather | solution.py:187
  836.0 631.3 %all-gather.24.cloned.1.call-done = bf16[2048,8192]{1,0:T(8,128)(2,1)} async-done(((bf16[512,8192]{1,0:T(8,128)(2,1)}), bf16[2048,8192]{1,0:T(8,128)(2,1)}) %all-gather.24.cloned.1.call-update) | async-done | bytes 33554448 | tf_op jit(solution)/shard_map/all_gather | solution.py:192
  1467.4 20.5 fusion.84
  1487.9 541.4 %all-gather.26.cloned.1.call-done = bf16[2048,8192]{1,0:T(8,128)(2,1)} async-done(((bf16[512,8192]{1,0:T(8,128)(2,1)}), bf16[2048,8192]{1,0:T(8,128)(2,1)}) %all-gather.26.cloned.1.call-update) | async-done | bytes 33554448 | tf_op jit(solution)/shard_map/all_gather | solution.py:193
  2029.3 21.3 fusion.85
  2057.4 622.8 %all-gather.28.cloned.1.call-done = bf16[2048,8192]{1,0:T(8,128)(2,1)} async-done(((bf16[512,8192]{1,0:T(8,128)(2,1)}), bf16[2048,8192]{1,0:T(8,128)(2,1)}) %all-gather.28.cloned.1.call-update) | async-done | bytes 33554448 | tf_op jit(solution)/shard_map/all_gather | solution.py:202
  2680.2 19.2 multiply_convert_fusion.1
  2699.4 16.3 fusion.86
  2715.7 16.6 multiply_reduce_fusion
  2747.5 246.4 %while.41 = (s32[]{:T(128)}, bf16[128,2048]{0,1:T(8,128)(2,1)}, bf16[128,2048]{0,1:T(8,128)(2,1)}, f32[128,2048]{0,1:T(8,128)}, f32[128,2048]{0,1:T(8,128)}, /*i...) while((s32[]{:T(128)}, bf16[128,2048]{0,1:T(8,128)(2,1)}, ...), condition=%wide.region_12.13_spmd.clone, body=%wide.region_10.12_spmd.clone.sunk | while | flops 342386304 | bytes 44634192 | solution.py:268
  2759.8 14.4 collective-permute-done.2
  3019.1 21.9 collective-permute-done.4
  3041.8 19.5 all-to-all-done.3
  3068.8 45.3 %all-to-all-done.2 = bf16[32,128,256]{2,1,0:T(8,128)(2,1)} async-done(((bf16[32,128,256]{2,1,0:T(8,128)(2,1)}), bf16[32,128,256]{2,1,0:T(8,128)(2,1)}, u32[]{:S(2)}, u32[]{:S(2)}) %all-to-all-start.2) | async-done | bytes 2097184 | tf_op jit(solution)/shard_map/all_to_all | solution.py:315
  3124.8 44.1 %all-to-all-done.1 = bf16[32,128,256]{2,1,0:T(8,128)(2,1)} async-done(((bf16[32,128,256]{2,1,0:T(8,128)(2,1)}), bf16[32,128,256]{2,1,0:T(8,128)(2,1)}, u32[]{:S(2)}, u32[]{:S(2)}) %all-to-all-start.1) | async-done | bytes 2097184 | tf_op jit(solution)/shard_map/all_to_all | solution.py:314
  3184.3 175.4 %all-to-all-done.8 = bf16[32,128,1024]{2,1,0:T(8,128)(2,1)} async-done(((bf16[32,128,1024]{2,1,0:T(8,128)(2,1)}), bf16[32,128,1024]{2,1,0:T(8,128)(2,1)}, u32[]{:S(2)}, u32[]{:S(2)}) %all-to-all-start.8) | async-done | bytes 8388640 | tf_op jit(solution)/shard_map/all_to_all | solution.py:319
  3376.3 178.8 %all-to-all-done.9 = bf16[32,128,1024]{1,2,0:T(8,128)(2,1)} async-done(((bf16[32,128,1024]{1,2,0:T(8,128)(2,1)}), bf16[32,128,1024]{1,2,0:T(8,128)(2,1)}, u32[]{:S(2)}, u32[]{:S(2)}) %all-to-all-start.9) | async-done | bytes 8388640 | tf_op jit(solution)/shard_map/all_to_all | solution.py:320
  3568.2 17.4 fusion.33
  3603.8 171.1 %psum.7 = f32[2,2048]{1,0:T(2,128)S(1)} all-reduce(f32[2,2048]{1,0:T(2,128)S(1)} %pad_maximum_fusion.3), channel_id=1, replica_groups=mesh['ctx'=8,'fsdp'=4] {'ctx','fsdp'}, use_global_device_ids=true, to_apply=%region_17.18 | all-reduce | flops 4096 | bytes 32768 | tf_op jit(solution)/shard_map/psum | solution.py:334
  (462 shorter events, 577.1 us)
Async XLA Ops:
  7.2 154.7 %all-gather.16.cloned.1.call-start = ((), (), s32[]{:S(2)}) async-start(), calls=%async_computation.13 | async-start | bytes 10485760 | tf_op jit(solution)/shard_map/all_gather | solution.py:145
  7.9 303.4 %all-gather.12.cloned.1.call-start = ((), (), s32[]{:S(2)}) async-start(), calls=%async_computation.11 | async-start | bytes 10485760 | tf_op jit(solution)/shard_map/all_gather | solution.py:146
  8.7 452.1 %all-gather.18.cloned.1.call-start = ((), (), s32[]{:S(2)}) async-start(), calls=%async_computation.14 | async-start | bytes 10485760 | tf_op jit(solution)/shard_map/all_gather | solution.py:147
  9.4 567.9 %all-gather.14.cloned.1.call-start = ((), (), s32[]{:S(2)}) async-start(), calls=%async_computation.12 | async-start | bytes 4718592 | tf_op jit(solution)/shard_map/all_gather | solution.py:169
  334.0 249.8 %all-gather.20.cloned.1.call-start = ((), (), s32[]{:S(2)}) async-start(), calls=%async_computation.15 | async-start | bytes 4718592 | tf_op jit(solution)/shard_map/all_gather | solution.py:170
  466.3 351.7 %all-gather.22.cloned.1.call-start = ((), (), s32[]{:S(2)}) async-start(), calls=%async_computation.16 | async-start | bytes 10485760 | tf_op jit(solution)/shard_map/all_gather | solution.py:187
  466.8 1000.5 %all-gather.24.cloned.1.call-start = ((), (), s32[]{:S(2)}) async-start(), calls=%async_computation.17 | async-start | bytes 41943040 | tf_op jit(solution)/shard_map/all_gather | solution.py:192
  467.6 1561.7 %all-gather.26.cloned.1.call-start = ((), (), s32[]{:S(2)}) async-start(), calls=%async_computation.18 | async-start | bytes 41943040 | tf_op jit(solution)/shard_map/all_gather | solution.py:193
  468.3 2211.9 %all-gather.28.cloned.1.call-start = ((), (), s32[]{:S(2)}) async-start(), calls=%async_computation.19 | async-start | bytes 41943040 | tf_op jit(solution)/shard_map/all_gather | solution.py:202
  473.6 134.6 %all-to-all-start = ((bf16[32,128,512]{1,2,0:T(8,128)(2,1)}), bf16[32,128,512]{1,2,0:T(8,128)(2,1)}, u32[]{:S(2)}, u32[]{:S(2)}) async-start(bf16[32,128,512]{1,2,0:T(8,128)(2,1)} %bitcast.333), calls=%async_computation | async-start | bytes 8388608 | tf_op jit(solution)/shard_map/all_to_all | solution.py:310
  610.8 214.9 %all-to-all-start.10 = ((bf16[32,128,512]{2,1,0:T(8,128)(2,1)}), bf16[32,128,512]{2,1,0:T(8,128)(2,1)}, u32[]{:S(2)}, u32[]{:S(2)}) async-start(bf16[32,128,512]{2,1,0:T(8,128)(2,1)} %bitcast.331), calls=%async_computation.10 | async-start | bytes 8388608 | tf_op jit(solution)/shard_map/all_to_all | solution.py:313
  829.7 1220.9 %all-to-all-start.6 = ((bf16[32,128,512]{1,2,0:T(8,128)(2,1)}), bf16[32,128,512]{1,2,0:T(8,128)(2,1)}, u32[]{:S(2)}, u32[]{:S(2)}) async-start(bf16[32,128,512]{1,2,0:T(8,128)(2,1)} %bitcast.334), calls=%async_computation.6 | async-start | bytes 8388608 | tf_op jit(solution)/shard_map/all_to_all | solution.py:312
  2053.5 688.7 %all-to-all-start.4 = ((bf16[32,128,512]{1,2,0:T(8,128)(2,1)}), bf16[32,128,512]{1,2,0:T(8,128)(2,1)}, u32[]{:S(2)}, u32[]{:S(2)}) async-start(bf16[32,128,512]{1,2,0:T(8,128)(2,1)} %bitcast.332), calls=%async_computation.4 | async-start | bytes 8388608 | tf_op jit(solution)/shard_map/all_to_all | solution.py:311
  2743.8 264.5 %all-to-all-start.5 = ((bf16[32,128,256]{2,1,0:T(8,128)(2,1)}), bf16[32,128,256]{2,1,0:T(8,128)(2,1)}, u32[]{:S(2)}, u32[]{:S(2)}) async-start(bf16[32,128,256]{2,1,0:T(8,128)(2,1)} %bitcast.49), calls=%async_computation.5 | async-start | bytes 4194304 | tf_op jit(solution)/shard_map/all_to_all | solution.py:317
  2754.8 28.6 collective-permute-start.3
  2756.4 36.6 collective-permute-start
  2756.5 43.0 %collective-permute-start.1 = (bf16[128,2048]{0,1:T(8,128)(2,1)S(1)}, bf16[128,2048]{0,1:T(8,128)(2,1)}, u32[]{:S(2)}, u32[]{:S(2)}) collective-permute-start(bf16[128,2048]{0,1:T(8,128)(2,1)S(1)} %copy.138), channel_id=1, source_target_pairs={{28,0},{0,4},{4,8},{8,12},{12,16},{16,20},{20,24},{24,28},{29,1},{... | collective-permute-start | bytes 1572872 | tf_op jit(solution)/shard_map/while/body/eval_jaxpr/ppermute | solution.py:18
  2806.6 25.3 collective-permute-start.1
  3010.9 50.4 %all-to-all-start.3 = ((bf16[32,128,256]{2,1,0:T(8,128)(2,1)}), bf16[32,128,256]{2,1,0:T(8,128)(2,1)}, u32[]{:S(2)}, u32[]{:S(2)}) async-start(bf16[32,128,256]{2,1,0:T(8,128)(2,1)} %bitcast.43), calls=%async_computation.3 | async-start | bytes 4194304 | tf_op jit(solution)/shard_map/all_to_all | solution.py:316
  3062.8 51.3 %all-to-all-start.2 = ((bf16[32,128,256]{2,1,0:T(8,128)(2,1)}), bf16[32,128,256]{2,1,0:T(8,128)(2,1)}, u32[]{:S(2)}, u32[]{:S(2)}) async-start(bf16[32,128,256]{2,1,0:T(8,128)(2,1)} %bitcast.39), calls=%async_computation.2 | async-start | bytes 4194304 | tf_op jit(solution)/shard_map/all_to_all | solution.py:315
  3116.7 52.1 %all-to-all-start.1 = ((bf16[32,128,256]{2,1,0:T(8,128)(2,1)}), bf16[32,128,256]{2,1,0:T(8,128)(2,1)}, u32[]{:S(2)}, u32[]{:S(2)}) async-start(bf16[32,128,256]{2,1,0:T(8,128)(2,1)} %bitcast.342), calls=%async_computation.1 | async-start | bytes 4194304 | tf_op jit(solution)/shard_map/all_to_all | solution.py:314
  3173.3 186.3 %all-to-all-start.8 = ((bf16[32,128,1024]{2,1,0:T(8,128)(2,1)}), bf16[32,128,1024]{2,1,0:T(8,128)(2,1)}, u32[]{:S(2)}, u32[]{:S(2)}) async-start(bf16[32,128,1024]{2,1,0:T(8,128)(2,1)} %bitcast.325), calls=%async_computation.8 | async-start | bytes 16777216 | tf_op jit(solution)/shard_map/all_to_all | solution.py:319
  3365.2 189.9 %all-to-all-start.9 = ((bf16[32,128,1024]{1,2,0:T(8,128)(2,1)}), bf16[32,128,1024]{1,2,0:T(8,128)(2,1)}, u32[]{:S(2)}, u32[]{:S(2)}) async-start(bf16[32,128,1024]{1,2,0:T(8,128)(2,1)} %bitcast.326), calls=%async_computation.9 | async-start | bytes 16777216 | tf_op jit(solution)/shard_map/all_to_all | solution.py:320
  3559.5 257.0 %all-to-all-start.7 = ((bf16[32,128,1024]{2,1,0:T(8,128)(2,1)}), bf16[32,128,1024]{2,1,0:T(8,128)(2,1)}, u32[]{:S(2)}, u32[]{:S(2)}) async-start(bf16[32,128,1024]{2,1,0:T(8,128)(2,1)} %bitcast.324), calls=%async_computation.7 | async-start | bytes 16777216 | tf_op jit(solution)/shard_map/all_to_all | solution.py:318
  (71 other events, 5205.9 us)
Sparse Core Ops, SparseCore 0:
  9.6 152.3 all-gather.15
  163.5 147.7 all-gather.11
  312.9 147.7 all-gather.17
  462.5 64.9 all-gather.13
  529.8 46.5 all-gather.19
  577.8 240.1 all-gather.21
  819.5 647.7 all-gather.23
  1468.9 560.3 all-gather.25
  2030.9 649.3 all-gather.27
where the time goes:
time: 3840 us; the launch traced here: 3830 us
  waiting for transfers between devices  2990 us (78%)
  blocking collectives  284 us (7%)
  matrix products  284 us (7%)
  local copies, waits for them, and re-layouts  131 us (3%)
  starting transfers between devices  72 us (2%)
  other arithmetic  56.6 us (1%)
    all_gather x1, waiting for transfers between devices, on_device(): piece_gate = lax.all_gather(w_gate, 'fsdp', axis=0, tiled=True)  631 us
    all_gather x1, waiting for transfers between devices, on_device(): lax.all_gather(w_down, 'fsdp', axis=0, tiled=True)  623 us
    all_gather x1, waiting for transfers between devices, on_device(): piece_up = lax.all_gather(w_up, 'fsdp', axis=0, tiled=True)  541 us
    all_to_all x1, waiting for transfers between devices, on_device(): lax.all_to_all(outgoing[10], ('ctx', 'fsdp'), split_axis=0, concat_axis=0...  179 us
    all_to_all x1, waiting for transfers between devices, on_device(): lax.all_to_all(outgoing[9], ('ctx', 'fsdp'), split_axis=0, concat_axis=0,...  175 us
    psum x1, blocking collectives, on_device(): lax.psum(jnp.stack([gain_grad_attn, gain_grad_mlp]), ('ctx', 'fsdp'))  171 us
    ppermute x30, waiting for transfers between devices, passed_along(): return lax.ppermute(block, axis, route)  163 us
    all_gather x1, waiting for transfers between devices, on_device(): lax.all_gather(w_out, 'fsdp', axis=0, tiled=True)  161 us
  transfers between devices with their start and end apart: 50, of which 42 were waited for; matrix products, arithmetic and copies ran while one was open for 11% of the time, Pallas kernels for 0%

commit v1 on v0

v1 whole, which is shorter than its diff:
```python
import jax
import jax.numpy as jnp
from jax import lax
from jax.sharding import PartitionSpec as P

HEADS = 32
HD = 64


eps = 1e-05
rope_base = 130000.0
neg_large = -1e30


def rms_scale(values):
    return lax.rsqrt(jnp.mean(values * values, axis=-1, keepdims=True) + eps)


def norm_back(grad_normed, normed, scaling):
    return scaling * (grad_normed - normed * jnp.mean(grad_normed * normed, axis=-1, keepdims=True))


def slot_positions(layout, row_ids, half_rows):
    slots = row_ids // half_rows
    onehot = slots[:, None] == jnp.arange(layout.shape[0], dtype=jnp.int32)[None, :]
    return jnp.sum(jnp.where(onehot, layout[None, :], 0), axis=1) * half_rows + row_ids % half_rows


def rotation_tables(positions, head_size):
    half_size = head_size // 2
    freqs = rope_base ** (-(jnp.arange(half_size, dtype=jnp.float32) * (2.0 / head_size)))
    angles = positions.astype(jnp.float32)[:, None] * freqs[None, :]
    cosine = jnp.concatenate([jnp.cos(angles), jnp.cos(angles)], axis=-1)[:, None, :]
    sine = jnp.concatenate([jnp.sin(angles), jnp.sin(angles)], axis=-1)[:, None, :]
    return (cosine, sine)


def rotate(values, cosine, sine):
    half_size = values.shape[-1] // 2
    turned = jnp.concatenate([-values[..., half_size:], values[..., :half_size]], axis=-1)
    return values * cosine + turned * sine


def rotate_back(grads, cosine, sine):
    half_size = grads.shape[-1] // 2
    scaled = grads * sine
    turned = jnp.concatenate([scaled[..., half_size:], -scaled[..., :half_size]], axis=-1)
    return grads * cosine + turned


def contract_last(left, right):
    return lax.dot_general(
        left, right, (((1,), (1,)), ((), ())), preferred_element_type=jnp.float32
    )


def own_columns(weight, place, size):
    share = weight.shape[1] // size
    return lax.dynamic_slice_in_dim(weight, place * share, share, 1)


def rows_gathered(part):
    return lax.all_gather(part, "fsdp", axis=0, tiled=True)


def contract_rows(left, right):
    return lax.dot_general(
        left, right, (((0,), (0,)), ((), ())), preferred_element_type=jnp.float32
    )


def plane_gather(part):
    return lax.all_gather(part, "ctx", axis=0, tiled=True)


def plane_scatter(total):
    return lax.psum_scatter(total.astype(jnp.bfloat16), "ctx", scatter_dimension=0, tiled=True).astype(
        jnp.float32
    )


def grads_scattered(total):
    return lax.psum_scatter(
        total.astype(jnp.bfloat16), "fsdp", scatter_dimension=0, tiled=True
    ).astype(jnp.float32)


def on_device(
    tokens,
    block_order,
    w_query,
    w_key,
    w_value,
    w_out,
    w_gate,
    w_up,
    w_down,
    norm_attn,
    norm_mlp,
    cotangent,
):
    inputs = tokens[0].astype(jnp.float32)
    tok_rows, model_width = inputs.shape
    head_size = HD
    scaling = head_size ** (-0.5)
    layout = block_order[0]
    ctx_size = lax.axis_size("ctx")
    ctx_place = lax.axis_index("ctx")
    fsdp_size = lax.axis_size("fsdp")
    fsdp_place = lax.axis_index("fsdp")
    seq_rows = tok_rows * ctx_size
    block_rows = seq_rows // layout.shape[0]
    own_heads = HEADS // ctx_size
    share = model_width // ctx_size
    positions = slot_positions(layout, jnp.arange(seq_rows, dtype=jnp.int32), block_rows)
    cosine, sine = rotation_tables(positions, head_size)

    gains = rows_gathered(jnp.stack([norm_attn, norm_mlp], axis=1)).astype(jnp.float32)
    gain_attn, gain_mlp = gains[:, 0], gains[:, 1]
    w_qkv = rows_gathered(
        jnp.concatenate([own_columns(w, ctx_place, ctx_size) for w in (w_query, w_key, w_value)], axis=1)
    )
    out_cols = rows_gathered(own_columns(w_out, ctx_place, ctx_size))
    out_rows = lax.all_to_all(out_cols, "ctx", split_axis=0, concat_axis=1, tiled=True)
    gate_cols = rows_gathered(own_columns(w_gate, ctx_place, ctx_size))
    up_cols = rows_gathered(own_columns(w_up, ctx_place, ctx_size))
    down_cols = rows_gathered(own_columns(w_down, ctx_place, ctx_size))

    scale_attn = rms_scale(inputs)
    normed_attn = inputs * scale_attn
    hidden_attn = plane_gather((normed_attn * gain_attn[None, :]).astype(jnp.bfloat16))
    grad_b = plane_gather(cotangent[0])
    qkv = jnp.dot(hidden_attn, w_qkv, preferred_element_type=jnp.float32)
    by_head = qkv.reshape(seq_rows, 3, own_heads, head_size)
    query_rot = rotate(by_head[:, 0], cosine, sine).astype(jnp.bfloat16)
    key_rot = rotate(by_head[:, 1], cosine, sine).astype(jnp.bfloat16)
    value_b = by_head[:, 2].astype(jnp.bfloat16)
    allowed = (positions[None, :] <= positions[:, None])[None]
    scores = jnp.einsum("qhd,khd->hqk", query_rot, key_rot, preferred_element_type=jnp.float32) * scaling
    maxima = jnp.max(jnp.where(allowed, scores, neg_large), axis=-1)
    probs = jnp.where(allowed, jnp.exp(scores - maxima[..., None]), 0.0)
    totals = jnp.sum(probs, axis=-1)
    mixed = jnp.einsum("hqk,khd->qhd", probs.astype(jnp.bfloat16), value_b, preferred_element_type=jnp.float32)
    attn_rows = (mixed / totals.T[:, :, None]).astype(jnp.bfloat16).reshape(seq_rows, share)
    log_totals = maxima + jnp.log(totals)

    mid_stream = inputs + plane_scatter(jnp.dot(attn_rows, out_rows, preferred_element_type=jnp.float32))
    scale_mlp = rms_scale(mid_stream)
    normed_mlp = mid_stream * scale_mlp
    hidden_mlp = plane_gather((normed_mlp * gain_mlp[None, :]).astype(jnp.bfloat16))
    gate_pre = jnp.dot(hidden_mlp, gate_cols, preferred_element_type=jnp.float32)
    up_pre = jnp.dot(hidden_mlp, up_cols, preferred_element_type=jnp.float32)
    sigmoid_gate = jax.nn.sigmoid(gate_pre)
    silu_gate = gate_pre * sigmoid_gate
    acted = (silu_gate * up_pre).astype(jnp.bfloat16)
    result = mid_stream + plane_scatter(contract_last(acted, down_cols))
    grad_down = grads_scattered(contract_rows(grad_b, acted))

    grad_act = jnp.dot(grad_b, down_cols, preferred_element_type=jnp.float32)
    grad_gate_pre = (
        grad_act * up_pre * sigmoid_gate * (1.0 + gate_pre * (1.0 - sigmoid_gate))
    ).astype(jnp.bfloat16)
    grad_up_pre = (grad_act * silu_gate).astype(jnp.bfloat16)
    grad_gate = grads_scattered(contract_rows(hidden_mlp, grad_gate_pre))
    grad_up = grads_scattered(contract_rows(hidden_mlp, grad_up_pre))
    columns = plane_scatter(contract_last(grad_gate_pre, gate_cols) + contract_last(grad_up_pre, up_cols))
    gain_grad_mlp = jnp.sum(columns * normed_mlp, axis=0)
    grad_mid = cotangent[0].astype(jnp.float32) + norm_back(
        columns * gain_mlp[None, :], normed_mlp, scale_mlp
    )
    grad_mid_b = plane_gather(grad_mid.astype(jnp.bfloat16))
    attn_all = lax.all_gather(attn_rows, "ctx", axis=1, tiled=True)
    grad_out = grads_scattered(contract_rows(attn_all, own_columns(grad_mid_b, ctx_place, ctx_size)))
    grad_attn = contract_last(grad_mid_b, out_rows).astype(jnp.bfloat16)
    delta = jnp.sum(
        (grad_attn.astype(jnp.float32) * attn_rows.astype(jnp.float32)).reshape(
            seq_rows, own_heads, head_size
        ),
        axis=-1,
    ).T
    grad_heads = grad_attn.reshape(seq_rows, own_heads, head_size)
    probs = jnp.where(allowed, jnp.exp(scores - log_totals[..., None]), 0.0)
    grad_v = jnp.einsum("hqk,qhd->khd", probs.astype(jnp.bfloat16), grad_heads, preferred_element_type=jnp.float32)
    grad_probs = jnp.einsum("qhd,khd->hqk", grad_heads, value_b, preferred_element_type=jnp.float32)
    grad_scores = (probs * (grad_probs - delta[..., None]) * scaling).astype(jnp.bfloat16)
    grad_q = jnp.einsum("hqk,khd->qhd", grad_scores, key_rot, preferred_element_type=jnp.float32)
    grad_k = jnp.einsum("hqk,qhd->khd", grad_scores, query_rot, preferred_element_type=jnp.float32)
    grad_qkv = jnp.stack(
        [
            rotate_back(grad_q, cosine, sine).astype(jnp.bfloat16),
            rotate_back(grad_k, cosine, sine).astype(jnp.bfloat16),
            grad_v.astype(jnp.bfloat16),
        ],
        axis=1,
    ).reshape(seq_rows, 3 * share)
    columns = plane_scatter(contract_last(grad_qkv, w_qkv))
    grads_qkv = grads_scattered(contract_rows(hidden_attn, grad_qkv))
    gain_grad_attn = jnp.sum(columns * normed_attn, axis=0)
    grad_input = grad_mid + norm_back(columns * gain_attn[None, :], normed_attn, scale_attn)
    gain_own = lax.psum(
        lax.psum_scatter(jnp.stack([gain_grad_attn, gain_grad_mlp], axis=1), "fsdp", scatter_dimension=0, tiled=True),
        "ctx",
    )
    return (
        result[None],
        grad_input[None],
        grads_qkv[:, :share],
        grads_qkv[:, share : 2 * share],
        grads_qkv[:, 2 * share :],
        grad_out,
        grad_gate,
        grad_up,
        grad_down,
        gain_own[:, 0],
        gain_own[:, 1],
    )


def solution(mesh):
    in_specs = (
        P("fsdp", "ctx", None),
        P("fsdp", None),
        P("fsdp", None),
        P("fsdp", None),
        P("fsdp", None),
        P("fsdp", None),
        P("fsdp", None),
        P("fsdp", None),
        P("fsdp", None),
        P("fsdp"),
        P("fsdp"),
        P("fsdp", "ctx", None),
    )
    out_specs = (
        P("fsdp", "ctx", None),
        P("fsdp", "ctx", None),
        P("fsdp", "ctx"),
        P("fsdp", "ctx"),
        P("fsdp", "ctx"),
        P("fsdp", "ctx"),
        P("fsdp", "ctx"),
        P("fsdp", "ctx"),
        P("fsdp", "ctx"),
        P("fsdp"),
        P("fsdp"),
    )
    return jax.shard_map(
        on_device, mesh=mesh, in_specs=in_specs, out_specs=out_specs, check_vma=False
    )
```

time: 3840 us -> 1200 us (0.31)
  waiting for transfers between devices: 2990 us -> 938 us
  blocking collectives: 284 us -> 27 us
  matrix products: 284 us -> 145 us
  local copies, waits for them, and re-layouts: 131 us -> 23.5 us
  starting transfers between devices: 72 us -> 5.65 us
    all_gather x9 -> x10, waiting for transfers between devices: 2360 us -> 412 us  [the longest x5 276 us: rows_gathered(): return lax.all_gather(part, 'fsdp', axis=0, tiled=True)]
    reduce_scatter x0 -> x9, waiting for transfers between devices: none -> 484 us  [the longest x5 281 us: grads_scattered(): lax.psum_scatter(total.astype(jnp.bfloat16), 'fsdp', scatter_dimension=0,...]
    all_to_all x11 -> x1, waiting for transfers between devices: 463 us -> 14 us  [on_device(): lax.all_to_all(out_cols, 'ctx', split_axis=0, concat_axis=1, tiled=True)]
    ppermute x30 -> x0, waiting for transfers between devices: 163 us -> none  [passed_along(): return lax.ppermute(block, axis, route)]
    psum x1, blocking collectives: 171 us -> 13.2 us  [on_device(): lax.psum(lax.psum_scatter(jnp.stack([gain_grad_attn, gain_grad_mlp], axis...]
    all_gather x2 -> x1, blocking collectives: 113 us -> 13.7 us  [rows_gathered(): return lax.all_gather(part, 'fsdp', axis=0, tiled=True)]
    dot_general x70 -> x16, matrix products: 208 us -> 116 us  [the longest x5 41 us: contract_rows(): lax.dot_general(left, right, (((0,), (0,)), ((), ())), preferred_element_...]
    all_to_all x11 -> x1, starting transfers between devices: 54.7 us -> 3.69 us  [on_device(): lax.all_to_all(out_cols, 'ctx', split_axis=0, concat_axis=1, tiled=True)]
  transfers between devices with their start and end apart: 50 -> 21, of which waited for: 42 -> 21; matrix products, arithmetic and copies ran while one was open for 11% -> 12% of each run, Pallas kernels for 0% -> 0%
where the time goes in v1:
time: 1200 us; the launch traced here: 1190 us
  waiting for transfers between devices  938 us (78%)
  matrix products  145 us (12%)
  other arithmetic  32.3 us (3%)
  blocking collectives  27 us (2%)
  local copies, waits for them, and re-layouts  23.5 us (2%)
  between operations  15.4 us (1%)
    reduce_scatter x5, waiting for transfers between devices, grads_scattered(): lax.psum_scatter(total.astype(jnp.bfloat16), 'fsdp', scatter_dimension=0,...  281 us
    all_gather x5, waiting for transfers between devices, rows_gathered(): return lax.all_gather(part, 'fsdp', axis=0, tiled=True)  276 us
    reduce_scatter x4, waiting for transfers between devices, plane_scatter(): lax.psum_scatter(total.astype(jnp.bfloat16), 'ctx', scatter_dimension=0,...  203 us
    all_gather x4, waiting for transfers between devices, plane_gather(): return lax.all_gather(part, 'ctx', axis=0, tiled=True)  119 us
    dot_general x5, matrix products, contract_rows(): lax.dot_general(left, right, (((0,), (0,)), ((), ())), preferred_element_...  41 us
    dot_general x5, matrix products, contract_last(): lax.dot_general(left, right, (((1,), (1,)), ((), ())), preferred_element_...  29.3 us
    unnamed x21, waiting for transfers between devices  28.6 us
  transfers between devices with their start and end apart: 21, of which 21 were waited for; matrix products, arithmetic and copies ran while one was open for 12% of the time, Pallas kernels for 0%

profile of v1, /device:TPU:0, one launch (start us, length us, event | category | flops | bytes accessed | tf_op | source)
XLA Modules:
  0.0 1187.0 jit_solution(6936991188948084828)
XLA Ops:
  12.7 13.7 %all_gather.33 = bf16[2048,2]{0,1:T(2,128)(2,1)S(1)} all-gather(bf16[512,2]{0,1:T(2,128)(2,1)S(1)} %pad_maximum_fusion.5), channel_id=1, replica_groups=mesh['ctx'=8,'fsdp'=4] {'fsdp'}, dimensions={0}, use_global_device_ids=true | all-gather | bytes 10240 | tf_op jit(solution)/shard_map/all_gather | solution.py:63
  27.8 13.2 %all-gather.16.cloned.1.call-done = bf16[2048,256]{1,0:T(8,128)(2,1)} async-done(((bf16[512,256]{1,0:T(8,128)(2,1)}), bf16[2048,256]{1,0:T(8,128)(2,1)}) %all-gather.16.cloned.1.call-update) | async-done | bytes 1048592 | tf_op jit(solution)/shard_map/all_gather | solution.py:63
  46.0 14.0 %all-to-all-done = bf16[8,256,256]{2,1,0:T(8,128)(2,1)S(1)} async-done(((bf16[8,256,256]{2,1,0:T(8,128)(2,1)}), bf16[8,256,256]{2,1,0:T(8,128)(2,1)S(1)}, u32[]{:S(2)}, u32[]{:S(2)}) %all-to-all-start) | async-done | bytes 1048608 | tf_op jit(solution)/shard_map/all_to_all | solution.py:124
  61.3 44.6 %all-gather.14.cloned.1.call-done = bf16[2048,768]{1,0:T(8,128)(2,1)} async-done(((bf16[512,768]{1,0:T(8,128)(2,1)}), bf16[2048,768]{1,0:T(8,128)(2,1)}) %all-gather.14.cloned.1.call-update) | async-done | bytes 3145744 | tf_op jit(solution)/shard_map/all_gather | solution.py:63
  105.9 37.7 %all-gather.12.cloned.1.call-done = bf16[1024,2048]{1,0:T(8,128)(2,1)} async-done(((bf16[128,2048]{1,0:T(8,128)(2,1)}), bf16[1024,2048]{1,0:T(8,128)(2,1)}) %all-gather.12.cloned.1.call-update) | async-done | bytes 4194320 | tf_op jit(solution)/shard_map/all_gather | solution.py:73
  171.1 48.9 %reduce-scatter.13.cloned.1.call-done = bf16[128,2048]{1,0:T(8,128)(2,1)} async-done(((bf16[1024,2048]{1,0:T(8,128)(2,1)}), bf16[128,2048]{1,0:T(8,128)(2,1)}) %reduce-scatter.13.cloned.1.call-update) | async-done | bytes 524304 | tf_op jit(solution)/shard_map/reduce_scatter | solution.py:77
  229.0 73.7 %all-gather.22.cloned.1.call-done = bf16[2048,1024]{1,0:T(8,128)(2,1)} async-done(((bf16[512,1024]{1,0:T(8,128)(2,1)}), bf16[2048,1024]{1,0:T(8,128)(2,1)}) %all-gather.22.cloned.1.call-update) | async-done | bytes 4194320 | tf_op jit(solution)/shard_map/all_gather | solution.py:63
  302.7 37.4 %all-gather.18.cloned.1.call-done = bf16[1024,2048]{1,0:T(8,128)(2,1)} async-done(((bf16[128,2048]{1,0:T(8,128)(2,1)}), bf16[1024,2048]{1,0:T(8,128)(2,1)}) %all-gather.18.cloned.1.call-update) | async-done | bytes 4194320 | tf_op jit(solution)/shard_map/all_gather | solution.py:73
  350.1 73.0 %all-gather.20.cloned.1.call-done = bf16[2048,1024]{1,0:T(8,128)(2,1)} async-done(((bf16[512,1024]{1,0:T(8,128)(2,1)}), bf16[2048,1024]{1,0:T(8,128)(2,1)}) %all-gather.20.cloned.1.call-update) | async-done | bytes 4194320 | tf_op jit(solution)/shard_map/all_gather | solution.py:63
  433.0 71.5 %all-gather.24.cloned.1.call-done = bf16[2048,1024]{1,0:T(8,128)(2,1)} async-done(((bf16[512,1024]{1,0:T(8,128)(2,1)}), bf16[2048,1024]{1,0:T(8,128)(2,1)}) %all-gather.24.cloned.1.call-update) | async-done | bytes 4194320 | tf_op jit(solution)/shard_map/all_gather | solution.py:63
  504.5 37.0 %all-gather.30.cloned.1.call-done = bf16[1,1024,2048]{2,1,0:T(8,128)(2,1)} async-done(((bf16[1,128,2048]{2,1,0:T(8,128)(2,1)}), bf16[1,1024,2048]{2,1,0:T(8,128)(2,1)}) %all-gather.30.cloned.1.call-update) | async-done | bytes 4194320 | tf_op jit(solution)/shard_map/all_gather | solution.py:73
  541.5 13.3 %fusion.12 = (bf16[1024,1024]{1,0:T(8,128)(2,1)S(1)}, bf16[1024,1024]{1,0:T(8,128)(2,1)S(1)}, bf16[1024,1024]{1,0:T(8,128)(2,1)}) fusion(f32[1024,1024]{1,0:T(8,128)} %fusion.83, f32[1024,1024]{1,0:T(8,128)} %fusion.84, bf16[2048,1024]{1,0:T(8,128)(2,1)} %all-gather.24.cloned.1.call-done, bf16[1,1024,2048]{2,1,0:T(8,128)(2,1)} %all-gather.30.cloned.1.call-done), kind=kOutput, calls=%fused_computation.17 | convolution fusion | flops 4310695936 | bytes 23068672 | tf_op jit(solution)/shard_map/dot_general | solution.py:159
  566.0 51.2 %reduce-scatter.17.cloned.1.call-done = bf16[128,2048]{1,0:T(8,128)(2,1)} async-done(((bf16[1024,2048]{1,0:T(8,128)(2,1)}), bf16[128,2048]{1,0:T(8,128)(2,1)}) %reduce-scatter.17.cloned.1.call-update) | async-done | bytes 524304 | tf_op jit(solution)/shard_map/reduce_scatter | solution.py:77
  641.0 10.2 convert_bitcast_fusion
  679.4 17.4 %all-gather.28.cloned.1.call-done = bf16[1024,2048]{0,1:T(8,128)(2,1)} async-done(((bf16[1024,256]{0,1:T(8,128)(2,1)}), bf16[1024,2048]{0,1:T(8,128)(2,1)}) %all-gather.28.cloned.1.call-update) | async-done | bytes 4194320 | tf_op jit(solution)/shard_map/all_gather | solution.py:172
  735.3 40.6 %reduce-scatter.25.cloned.1.call-done = bf16[512,1024]{1,0:T(8,128)(2,1)} async-done(((bf16[2048,1024]{1,0:T(8,128)(2,1)}), bf16[512,1024]{1,0:T(8,128)(2,1)}) %reduce-scatter.25.cloned.1.call-update) | async-done | bytes 1048592 | tf_op jit(solution)/shard_map/reduce_scatter | solution.py:83
  778.7 76.7 %reduce-scatter.27.cloned.1.call-done = bf16[512,1024]{1,0:T(8,128)(2,1)} async-done(((bf16[2048,1024]{1,0:T(8,128)(2,1)}), bf16[512,1024]{1,0:T(8,128)(2,1)}) %reduce-scatter.27.cloned.1.call-update) | async-done | bytes 1048592 | tf_op jit(solution)/shard_map/reduce_scatter | solution.py:83
  858.2 76.7 %reduce-scatter.29.cloned.1.call-done = bf16[512,1024]{0,1:T(8,128)(2,1)} async-done(((bf16[2048,1024]{0,1:T(8,128)(2,1)}), bf16[512,1024]{0,1:T(8,128)(2,1)}) %reduce-scatter.29.cloned.1.call-update) | async-done | bytes 1048592 | tf_op jit(solution)/shard_map/reduce_scatter | solution.py:83
  937.4 28.0 %reduce-scatter.23.cloned.1.call-done = bf16[512,256]{1,0:T(8,128)(2,1)} async-done(((bf16[2048,256]{1,0:T(8,128)(2,1)}), bf16[512,256]{1,0:T(8,128)(2,1)}) %reduce-scatter.23.cloned.1.call-update) | async-done | bytes 262160 | tf_op jit(solution)/shard_map/reduce_scatter | solution.py:83
  967.2 51.1 %reduce-scatter.19.cloned.1.call-done = bf16[128,2048]{1,0:T(8,128)(2,1)} async-done(((bf16[1024,2048]{1,0:T(8,128)(2,1)}), bf16[128,2048]{1,0:T(8,128)(2,1)}) %reduce-scatter.19.cloned.1.call-update) | async-done | bytes 524304 | tf_op jit(solution)/shard_map/reduce_scatter | solution.py:77
  1021.2 51.5 %reduce-scatter.15.cloned.1.call-done = bf16[128,2048]{1,0:T(8,128)(2,1)} async-done(((bf16[1024,2048]{1,0:T(8,128)(2,1)}), bf16[128,2048]{1,0:T(8,128)(2,1)}) %reduce-scatter.15.cloned.1.call-update) | async-done | bytes 524304 | tf_op jit(solution)/shard_map/reduce_scatter | solution.py:77
  1076.4 59.1 %reduce-scatter.21.cloned.1.call-done = bf16[512,768]{1,0:T(8,128)(2,1)} async-done(((bf16[2048,768]{1,0:T(8,128)(2,1)}), bf16[512,768]{1,0:T(8,128)(2,1)}) %reduce-scatter.21.cloned.1.call-update) | async-done | bytes 786448 | tf_op jit(solution)/shard_map/reduce_scatter | solution.py:83
  1137.8 27.1 %reduce-scatter.31.cloned.1.call-done = f32[512,2]{1,0:T(8,128)} async-done(((f32[2048,2]{1,0:T(8,128)}), f32[512,2]{1,0:T(8,128)}) %reduce-scatter.31.cloned.1.call-update) | async-done | bytes 4112
  1165.9 13.2 %psum.7 = f32[512,2]{0,1:T(2,128)S(1)} all-reduce(f32[512,2]{0,1:T(2,128)S(1)} %copy.68), channel_id=1, replica_groups=mesh['ctx'=8,'fsdp'=4] {'ctx'}, use_global_device_ids=true, to_apply=%region_20.21 | all-reduce | flops 1024 | bytes 8192 | tf_op jit(solution)/shard_map/psum | solution.py:200
  (173 shorter events, 190.9 us)
Async XLA Ops:
  7.2 33.7 %all-gather.16.cloned.1.call-start = ((), (), s32[]{:S(2)}) async-start(), calls=%async_computation.13 | async-start | bytes 1310720 | tf_op jit(solution)/shard_map/all_gather | solution.py:63
  9.5 96.4 %all-gather.14.cloned.1.call-start = ((), (), s32[]{:S(2)}) async-start(), calls=%async_computation.12 | async-start | bytes 3932160 | tf_op jit(solution)/shard_map/all_gather | solution.py:63
  12.6 131.1 %all-gather.12.cloned.1.call-start = ((), (), s32[]{:S(2)}) async-start(), calls=%async_computation.11 | async-start | bytes 4718592 | tf_op jit(solution)/shard_map/all_gather | solution.py:73
  41.0 19.1 %all-to-all-start = ((bf16[8,256,256]{2,1,0:T(8,128)(2,1)}), bf16[8,256,256]{2,1,0:T(8,128)(2,1)S(1)}, u32[]{:S(2)}, u32[]{:S(2)}) async-start(bf16[8,256,256]{2,1,0:T(8,128)(2,1)} %bitcast.144), calls=%async_computation | async-start | bytes 2097152 | tf_op jit(solution)/shard_map/all_to_all | solution.py:124
  44.6 175.3 %reduce-scatter.13.cloned.1.call-start = ((), (), s32[]{:S(2)}) async-start(), calls=%async_computation.14 | async-start | bytes 4718592 | tf_op jit(solution)/shard_map/reduce_scatter | solution.py:77
  168.7 134.0 %all-gather.22.cloned.1.call-start = ((), (), s32[]{:S(2)}) async-start(), calls=%async_computation.17 | async-start | bytes 5242880 | tf_op jit(solution)/shard_map/all_gather | solution.py:63
  171.0 169.1 %all-gather.18.cloned.1.call-start = ((), (), s32[]{:S(2)}) async-start(), calls=%async_computation.15 | async-start | bytes 4718592 | tf_op jit(solution)/shard_map/all_gather | solution.py:73
  223.3 199.7 %all-gather.20.cloned.1.call-start = ((), (), s32[]{:S(2)}) async-start(), calls=%async_computation.16 | async-start | bytes 5242880 | tf_op jit(solution)/shard_map/all_gather | solution.py:63
  225.7 278.8 %all-gather.24.cloned.1.call-start = ((), (), s32[]{:S(2)}) async-start(), calls=%async_computation.18 | async-start | bytes 5242880 | tf_op jit(solution)/shard_map/all_gather | solution.py:63
  228.0 313.4 %all-gather.30.cloned.1.call-start = ((), (), s32[]{:S(2)}) async-start(), calls=%async_computation.29 | async-start | bytes 4718592 | tf_op jit(solution)/shard_map/all_gather | solution.py:73
  228.8 388.5 %reduce-scatter.17.cloned.1.call-start = ((), (), s32[]{:S(2)}) async-start(), calls=%async_computation.20 | async-start | bytes 4718592 | tf_op jit(solution)/shard_map/reduce_scatter | solution.py:77
  566.0 91.9 %all-gather.26.cloned.1.call-start = ((), (), s32[]{:S(2)}) async-start(), calls=%async_computation.21 | async-start | bytes 4718592 | tf_op jit(solution)/shard_map/all_gather | solution.py:73
  621.1 75.7 %all-gather.28.cloned.1.call-start = ((), (), s32[]{:S(2)}) async-start(), calls=%async_computation.24 | async-start | bytes 4718592 | tf_op jit(solution)/shard_map/all_gather | solution.py:172
  621.7 154.2 %reduce-scatter.25.cloned.1.call-start = ((), (), s32[]{:S(2)}) async-start(), calls=%async_computation.26 | async-start | bytes 5242880 | tf_op jit(solution)/shard_map/reduce_scatter | solution.py:83
  631.3 224.1 %reduce-scatter.27.cloned.1.call-start = ((), (), s32[]{:S(2)}) async-start(), calls=%async_computation.27 | async-start | bytes 5242880 | tf_op jit(solution)/shard_map/reduce_scatter | solution.py:83
  640.9 293.9 %reduce-scatter.29.cloned.1.call-start = ((), (), s32[]{:S(2)}) async-start(), calls=%async_computation.28 | async-start | bytes 5242880 | tf_op jit(solution)/shard_map/reduce_scatter | solution.py:83
  651.2 314.2 %reduce-scatter.23.cloned.1.call-start = ((), (), s32[]{:S(2)}) async-start(), calls=%async_computation.25 | async-start | bytes 1310720 | tf_op jit(solution)/shard_map/reduce_scatter | solution.py:83
  701.3 317.0 %reduce-scatter.19.cloned.1.call-start = ((), (), s32[]{:S(2)}) async-start(), calls=%async_computation.22 | async-start | bytes 4718592 | tf_op jit(solution)/shard_map/reduce_scatter | solution.py:77
  718.0 354.7 %reduce-scatter.15.cloned.1.call-start = ((), (), s32[]{:S(2)}) async-start(), calls=%async_computation.19 | async-start | bytes 4718592 | tf_op jit(solution)/shard_map/reduce_scatter | solution.py:77
  727.5 408.0 %reduce-scatter.21.cloned.1.call-start = ((), (), s32[]{:S(2)}) async-start(), calls=%async_computation.23 | async-start | bytes 3932160 | tf_op jit(solution)/shard_map/reduce_scatter | solution.py:83
  735.0 429.8 %reduce-scatter.31.cloned.1.call-start = ((), (), s32[]{:S(2)}) async-start(), calls=%async_computation.30 | async-start | bytes 1310720
  778.7 239.6 %copy-start.18 = (f32[2048,1]{0,1:T(1,128)S(1)}, f32[2048,1]{0,1:T(1,128)}, u32[]{:S(2)}) copy-start(f32[2048,1]{0,1:T(1,128)} %copy-done.17) | copy-start | bytes 24580
  778.7 239.6 %copy-start.20 = (f32[128]{0:T(128)S(1)}, f32[128]{0:T(128)}, u32[]{:S(2)}) copy-start(f32[128]{0:T(128)} %copy-done.19) | copy-start | bytes 1540
  1021.2 158.5 %copy-start.1 = (bf16[512,2048]{1,0:T(8,128)(2,1)S(1)}, bf16[512,2048]{1,0:T(8,128)(2,1)}, u32[]{:S(2)}) copy-start(bf16[512,2048]{1,0:T(8,128)(2,1)} %param.17) | copy-start | bytes 6291460
  (28 other events, 511.4 us)
Sparse Core Ops, SparseCore 0:
  10.2 30.7 all-gather.15
  43.1 62.7 all-gather.13
  108.4 35.2 all-gather.11
  168.8 51.1 reduce-scatter.12
  222.0 80.7 all-gather.21
  305.0 35.0 all-gather.17
  342.3 80.7 all-gather.19
  425.2 79.2 all-gather.23
  506.4 35.0 all-gather.29
  566.1 51.1 reduce-scatter.16
  621.2 36.5 all-gather.25
  660.2 36.5 all-gather.27
  699.1 76.7 reduce-scatter.24
  778.1 77.2 reduce-scatter.26
  857.5 77.2 reduce-scatter.28
  937.6 27.8 reduce-scatter.22
  968.6 49.6 reduce-scatter.18
  1021.5 51.1 reduce-scatter.14
  1075.0 60.3 reduce-scatter.20
  1137.6 27.1 reduce-scatter.30

commit v2 on v1

v2 whole, which is shorter than its diff:
```python
import jax
import jax.numpy as jnp
from jax import lax
from jax.experimental import pallas as pl
from jax.experimental.pallas import tpu as pltpu
from jax.sharding import PartitionSpec as P


HEADS = 32
HD = 64


eps = 1e-05
rope_base = 130000.0
neg_large = -1e30


def rms_scale(values):
    return lax.rsqrt(jnp.mean(values * values, axis=-1, keepdims=True) + eps)


def norm_back(grad_normed, normed, scaling):
    return scaling * (grad_normed - normed * jnp.mean(grad_normed * normed, axis=-1, keepdims=True))


def slot_positions(layout, row_ids, half_rows):
    slots = row_ids // half_rows
    onehot = slots[:, None] == jnp.arange(layout.shape[0], dtype=jnp.int32)[None, :]
    return jnp.sum(jnp.where(onehot, layout[None, :], 0), axis=1) * half_rows + row_ids % half_rows


def rotation_tables(positions, head_size):
    half_size = head_size // 2
    freqs = rope_base ** (-(jnp.arange(half_size, dtype=jnp.float32) * (2.0 / head_size)))
    angles = positions.astype(jnp.float32)[:, None] * freqs[None, :]
    cosine = jnp.concatenate([jnp.cos(angles), jnp.cos(angles)], axis=-1)[:, None, :]
    sine = jnp.concatenate([jnp.sin(angles), jnp.sin(angles)], axis=-1)[:, None, :]
    return (cosine, sine)


def rotate(values, cosine, sine):
    half_size = values.shape[-1] // 2
    turned = jnp.concatenate([-values[..., half_size:], values[..., :half_size]], axis=-1)
    return values * cosine + turned * sine


def rotate_back(grads, cosine, sine):
    half_size = grads.shape[-1] // 2
    scaled = grads * sine
    turned = jnp.concatenate([scaled[..., half_size:], -scaled[..., :half_size]], axis=-1)
    return grads * cosine + turned


def contract_last(left, right):
    return lax.dot_general(
        left, right, (((1,), (1,)), ((), ())), preferred_element_type=jnp.float32
    )


def own_columns(weight, place, size):
    share = weight.shape[1] // size
    return lax.dynamic_slice_in_dim(weight, place * share, share, 1)


def rows_gathered(part):
    return lax.all_gather(part, "fsdp", axis=0, tiled=True)


def contract_rows(left, right):
    return lax.dot_general(
        left, right, (((0,), (0,)), ((), ())), preferred_element_type=jnp.float32
    )


def send(source, target, sems, slot, peer):
    send_sems, recv_sems = sems
    return pltpu.make_async_remote_copy(
        src_ref=source,
        dst_ref=target,
        send_sem=send_sems.at[slot],
        recv_sem=recv_sems.at[slot],
        device_id=peer,
        device_id_type=pl.DeviceIdType.MESH,
    )


def greet(peers):
    barrier = pltpu.get_barrier_semaphore()
    for peer in peers:
        pl.semaphore_signal(barrier, inc=1, device_id=peer, device_id_type=pl.DeviceIdType.MESH)
    pl.semaphore_wait(barrier, len(peers))


def plane_peers():
    me = lax.axis_index("ctx")
    z = lax.axis_index("fsdp")
    return me, z, (me ^ 1, z), (me ^ 2, z), (me ^ 4, z)


def gather_copies(part, whole, me, core, x, y, sems, base):
    half = part.shape[0] // 2
    first, last = pl.ds(0, half), pl.ds(half, half)

    def block(owner, rows):
        return whole.at[owner, rows]

    own = [
        send(part.at[first], block(me, first), sems, base + 0, y),
        send(part.at[last], block(me, last), sems, base + 1, x),
        send(part.at[last], block(me, last), sems, base + 2, y),
        send(part.at[first], block(me, first), sems, base + 3, x),
        send(part, whole.at[me], sems, base + 4, core),
    ]
    along_x = send(block(me ^ 4, first), block(me ^ 4, first), sems, base + 5, x)
    along_y = send(block(me ^ 2, last), block(me ^ 2, last), sems, base + 6, y)
    to_core = [
        send(whole.at[me ^ 4], whole.at[me ^ 4], sems, base + 7, core),
        send(whole.at[me ^ 2], whole.at[me ^ 2], sems, base + 8, core),
        send(block(me ^ 6, first), block(me ^ 6, first), sems, base + 9, core),
        send(block(me ^ 6, last), block(me ^ 6, last), sems, base + 10, core),
    ]
    return own, along_x, along_y, to_core


GATHER_COPIES = 11


def plane_gather_steps(parts, wholes, place, sems, kept_sems):
    me, _, core, x, y = place
    plans = [
        gather_copies(parts[i], wholes[i], me, core, x, y, sems, i * GATHER_COPIES) for i in range(len(parts))
    ]
    kept = [
        pltpu.make_async_copy(parts[i], wholes[i].at[me], kept_sems.at[i]) for i in range(len(parts))
    ]

    def begin():
        for plan in plans:
            for copy in plan[0]:
                copy.start()
        for copy in kept:
            copy.start()

    def turn(own, along_x, along_y, to_core):
        own[0].wait_recv()
        along_x.start()
        own[1].wait_recv()
        along_y.start()
        own[2].wait_recv()
        to_core[0].start()
        own[3].wait_recv()
        to_core[1].start()

    def share(own, along_x, along_y, to_core):
        along_x.wait_recv()
        to_core[2].start()
        along_y.wait_recv()
        to_core[3].start()

    def end():
        for own, along_x, along_y, to_core in plans:
            own[4].wait_recv()
            for copy in to_core:
                copy.wait_recv()
            for copy in own + [along_x, along_y] + to_core:
                copy.wait_send()
        for copy in kept:
            copy.wait()

    steps = [begin]
    steps += [lambda plan=plan: turn(*plan) for plan in plans]
    steps += [lambda plan=plan: share(*plan) for plan in plans]
    return steps, end


def line_gather_steps(size, parts, wholes, place, sems, kept_sems):
    ctx, me = place[0], place[1]
    send_sems, recv_sems = sems
    kept = [
        pltpu.make_async_copy(parts[i], wholes[i].at[me], kept_sems.at[i]) for i in range(len(parts))
    ]

    def passing(i, upward, dist, source, owner):
        return pltpu.make_async_remote_copy(
            src_ref=source,
            dst_ref=wholes[i].at[owner],
            send_sem=send_sems.at[i, upward, dist],
            recv_sem=recv_sems.at[i, upward, dist],
            device_id=(ctx, me + (1 if upward else -1)),
            device_id_type=pl.DeviceIdType.MESH,
        )

    def sends(upward, dist):
        return ((me < size - 1) & (me >= dist - 1)) if upward else ((me > 0) & (me <= size - dist))

    def step(dist):
        for i in range(len(parts)):
            for upward in (1, 0):
                owner = me - (dist - 1) if upward else me + (dist - 1)

                @pl.when(sends(upward, dist))
                def _():
                    if dist > 1:
                        passing(i, upward, dist - 1, parts[i], owner).wait_recv()
                        passing(i, upward, dist, wholes[i].at[owner], owner).start()
                    else:
                        passing(i, upward, dist, parts[i], owner).start()

        if dist == 1:
            for copy in kept:
                copy.start()

    def end():
        for i in range(len(parts)):
            for upward, last in ((1, size - 1), (0, 0)):
                @pl.when(me == (last if upward else 0))
                def _():
                    for dist in range(1, size):
                        passing(i, upward, dist, parts[i], me).wait_recv()

                for dist in range(1, size):

                    @pl.when(sends(upward, dist))
                    def _():
                        passing(i, upward, dist, parts[i], me).wait_send()

        for copy in kept:
            copy.wait()

    return [lambda dist=dist: step(dist) for dist in range(1, size)], end


def line_spread_steps(size, source, part, whole, place, sems, kept_sem, pieces=4):
    ctx, me = place[0], place[1]
    send_sems, recv_sems = sems
    rows = whole.shape[0] // pieces

    def passing(piece, upward, origin):
        span = pl.ds(piece * rows, rows)
        return pltpu.make_async_remote_copy(
            src_ref=origin.at[span],
            dst_ref=whole.at[span],
            send_sem=send_sems.at[upward, piece],
            recv_sem=recv_sems.at[upward, piece],
            device_id=(ctx, me + (1 if upward else -1)),
            device_id_type=pl.DeviceIdType.MESH,
        )

    kept = pltpu.make_async_copy(part, whole, kept_sem)

    def sends(upward):
        return ((me >= source) & (me < size - 1)) if upward else ((me <= source) & (me > 0))

    def begin():
        for upward in (1, 0):

            @pl.when((me == source) & sends(upward))
            def _():
                for piece in range(pieces):
                    passing(piece, upward, part).start()

        @pl.when(me == source)
        def _():
            kept.start()

    def onward(hops):
        for upward in (1, 0):

            @pl.when((me == source + hops) if upward else (me == source - hops))
            def _():
                for piece in range(pieces):
                    passing(piece, upward, whole).wait_recv()

                    @pl.when(sends(upward))
                    def _():
                        passing(piece, upward, whole).start()

    def end():
        for upward in (1, 0):

            @pl.when(sends(upward))
            def _():
                for piece in range(pieces):
                    passing(piece, upward, whole).wait_send()

        @pl.when(me == source)
        def _():
            kept.wait()

    return [begin] + [lambda hops=hops: onward(hops) for hops in range(1, size)], end


def line_scatter_steps(size, arrays, outs, arrived, running, place, sems):
    ctx, me = place[0], place[1]
    send_sems, recv_sems = sems
    count, rows = len(arrays), outs[0].shape[0]

    def part(i, owner):
        return arrays[i].at[pl.ds(owner * rows, rows)]

    def passing(i, owner, upward, source):
        return pltpu.make_async_remote_copy(
            src_ref=source,
            dst_ref=arrived[i].at[upward, owner],
            send_sem=send_sems.at[i, upward, owner],
            recv_sem=recv_sems.at[i, upward, owner],
            device_id=(ctx, me + (1 if upward else -1)),
            device_id_type=pl.DeviceIdType.MESH,
        )

    def way(step, upward):
        owner = size - 1 - step if upward else step
        return owner, (me < owner) if upward else (me > owner), 0 if upward else size - 1

    def forward(i, step, upward, slot):
        owner, passes, first = way(step, upward)
        passes = passes & ((me if upward else size - 1 - me) == slot - 1 - step)

        @pl.when(passes & (me == first))
        def _():
            passing(i, owner, upward, part(i, owner)).start()

        @pl.when(passes & (me != first))
        def _():
            passing(i, owner, upward, part(i, owner)).wait_recv()
            add_rows(running[i].at[owner], part(i, owner), arrived[i].at[upward, owner], jnp.bfloat16)
            passing(i, owner, upward, running[i].at[owner]).start()

    def turn(slot):
        for i in range(count):
            for upward in (1, 0):
                for step in range(slot):
                    forward(i, step, upward, slot)

    def end():
        for i in range(count):
            for owner in range(size):
                ways = [upward for upward in (1, 0) if owner != (0 if upward else size - 1)]
                for upward in ways:
                    source = part(i, owner) if upward == ways[0] else outs[i]

                    @pl.when(me == owner)
                    def _():
                        passing(i, owner, upward, part(i, owner)).wait_recv()
                        add_rows(outs[i], source, arrived[i].at[upward, owner], jnp.float32)

        for i in range(count):
            for step in range(size - 1):
                for upward in (1, 0):
                    owner, passes, _ = way(step, upward)

                    @pl.when(passes)
                    def _():
                        passing(i, owner, upward, part(i, owner)).wait_send()

    return [lambda slot=slot: turn(slot) for slot in range(size)], end


def greet_line(place, size, peers):
    ctx, me = place[0], place[1]
    barrier = pltpu.get_barrier_semaphore()
    for way, edge in ((-1, 0), (1, size - 1)):

        @pl.when(me != edge)
        def _():
            pl.semaphore_signal(
                barrier, inc=1, device_id=(ctx, me + way), device_id_type=pl.DeviceIdType.MESH
            )

    for peer in peers:
        pl.semaphore_signal(barrier, inc=1, device_id=peer, device_id_type=pl.DeviceIdType.MESH)
    pl.semaphore_wait(barrier, len(peers) + jnp.where((me == 0) | (me == size - 1), 1, 2))


def run_steps(plans):
    longest = max(len(steps) for steps, end in plans)
    for k in range(longest):
        for steps, end in plans:
            if k < len(steps):
                steps[k]()
    for steps, end in plans:
        end()


def dma(*shape):
    return pltpu.SemaphoreType.DMA(shape)


def on_grid():
    return lax.axis_size("ctx") == 8 and lax.axis_size("fsdp") == 4


def plane_gather(parts, ident):
    if lax.axis_size("ctx") != 8:
        return [lax.all_gather(part, "ctx", axis=0, tiled=True) for part in parts]
    count = len(parts)

    def kernel(*refs):
        ins, outs = refs[:count], refs[count : 2 * count]
        place = plane_peers()
        greet(place[2:])
        run_steps([plane_gather_steps(ins, outs, place, refs[2 * count : 2 * count + 2], refs[2 * count + 2])])

    wholes = pl.pallas_call(
        kernel,
        out_shape=[jax.ShapeDtypeStruct((8,) + part.shape, part.dtype) for part in parts],
        in_specs=[pl.BlockSpec(memory_space=pltpu.VMEM)] * count,
        out_specs=[pl.BlockSpec(memory_space=pl.ANY)] * count,
        scratch_shapes=[dma(count * GATHER_COPIES), dma(count * GATHER_COPIES), dma(count)],
        compiler_params=pltpu.CompilerParams(collective_id=ident, has_side_effects=True),
        name="plane_gather",
    )(*parts)
    return [whole.reshape((-1,) + whole.shape[2:]) for whole in wholes]


def first_gather(parts, lined, out_part, ident):
    size = lax.axis_size("fsdp")
    if not on_grid():
        wholes = [lax.all_gather(part, "ctx", axis=0, tiled=True) for part in parts]
        return wholes + [lax.all_gather(part, "fsdp", axis=0) for part in lined] + [None]
    count, extra = len(parts), len(lined)
    total = count + extra + 1

    def kernel(*refs):
        ins, outs = refs[:total], refs[total : 2 * total]
        plane_send, plane_recv, line_send, line_recv, spread_send, spread_recv, kept = refs[2 * total :]
        place = plane_peers()
        source = place[0] * size // 8
        line = (place[0], place[1])
        greet_line(line, size, place[2:])
        run_steps(
            [
                line_gather_steps(
                    size,
                    ins[count : total - 1],
                    outs[count : total - 1],
                    line,
                    (line_send, line_recv),
                    kept.at[pl.ds(count, extra)],
                ),
                line_spread_steps(
                    size, source, ins[-1], outs[-1], line, (spread_send, spread_recv), kept.at[total - 1]
                ),
                plane_gather_steps(ins[:count], outs[:count], place, (plane_send, plane_recv), kept),
            ]
        )

    shapes = [(8,) + part.shape for part in parts] + [(size,) + part.shape for part in lined] + [out_part.shape]
    results = pl.pallas_call(
        kernel,
        out_shape=[jax.ShapeDtypeStruct(shape, jnp.bfloat16) for shape in shapes],
        in_specs=[pl.BlockSpec(memory_space=pltpu.VMEM)] * total,
        out_specs=[pl.BlockSpec(memory_space=pl.ANY)] * total,
        scratch_shapes=[
            dma(count * GATHER_COPIES),
            dma(count * GATHER_COPIES),
            dma(extra, 2, size),
            dma(extra, 2, size),
            dma(2, 4),
            dma(2, 4),
            dma(total),
        ],
        compiler_params=pltpu.CompilerParams(collective_id=ident, has_side_effects=True),
        name="first_gather",
    )(*parts, *lined, out_part)
    wholes = [whole.reshape((-1,) + whole.shape[2:]) for whole in results[:count]]
    return wholes + list(results[count:])


def swap(weights, totals, ident):
    size = lax.axis_size("fsdp")
    if not on_grid():
        return [rows_gathered(weight) for weight in weights], [offloaded_scatter(total) for total in totals]
    given, count = len(weights), len(totals)
    shards = [(total.shape[0] // size, total.shape[1]) for total in totals]

    def kernel(*refs):
        parts, arrays = refs[:given], refs[given : given + count]
        wholes, outs = refs[given + count : 2 * given + count], refs[2 * given + count : 2 * (given + count)]
        arrived, running = (refs[2 * given + k * count : 2 * given + (k + 1) * count] for k in (2, 3))
        gather_send, gather_recv, kept, send_sems, recv_sems = refs[2 * given + 4 * count :]
        place = (lax.axis_index("ctx"), lax.axis_index("fsdp"))
        greet_line(place, size, ())
        run_steps(
            [
                line_gather_steps(size, parts, wholes, place, (gather_send, gather_recv), kept),
                line_scatter_steps(size, arrays, outs, arrived, running, place, (send_sems, recv_sems)),
            ]
        )

    results = pl.pallas_call(
        kernel,
        out_shape=[jax.ShapeDtypeStruct((size,) + weight.shape, weight.dtype) for weight in weights]
        + [jax.ShapeDtypeStruct(shard, jnp.float32) for shard in shards],
        in_specs=[pl.BlockSpec(memory_space=pltpu.VMEM)] * (given + count),
        out_specs=[pl.BlockSpec(memory_space=pl.ANY)] * given + [pl.BlockSpec(memory_space=pltpu.VMEM)] * count,
        scratch_shapes=[pltpu.VMEM((2, size) + shard, jnp.bfloat16) for shard in shards]
        + [pltpu.VMEM((size,) + shard, jnp.bfloat16) for shard in shards]
        + [dma(given, 2, size), dma(given, 2, size), dma(given), dma(count, 2, size), dma(count, 2, size)],
        compiler_params=pltpu.CompilerParams(collective_id=ident, has_side_effects=True),
        name="swap",
    )(*weights, *totals)
    return [whole.reshape(-1, whole.shape[2]) for whole in results[:given]], list(results[given:])


def add_rows(target, left, right, kind, step=32):
    def one(turn, carried):
        rows = pl.ds(pl.multiple_of(turn * step, step), step)
        target[rows] = (left[rows].astype(jnp.float32) + right[rows].astype(jnp.float32)).astype(kind)
        return carried

    lax.fori_loop(0, target.shape[0] // step, one, 0)


def scatter_kernel(total, out, near, sums, far, send_sems, recv_sems):
    sems = (send_sems, recv_sems)
    me, _, core, x, y = plane_peers()
    greet((core, x, y))
    rows = out.shape[0]
    half = rows // 2
    first, last = pl.ds(0, half), pl.ds(half, half)
    flips = (6, 2, 4, 0)
    inward = [send(total.at[me ^ 1 ^ flip], near.at[i], sems, i, core) for i, flip in enumerate(flips)]
    for copy in inward:
        copy.start()
    diagonal_x = send(sums.at[0, first], far.at[0, first], sems, 4, x)
    diagonal_y = send(sums.at[0, last], far.at[0, last], sems, 5, y)
    x_first = send(sums.at[1, first], far.at[1, first], sems, 6, x)
    x_last = send(sums.at[1, last], far.at[1, last], sems, 7, x)
    y_first = send(sums.at[2, first], far.at[2, first], sems, 8, y)
    y_last = send(sums.at[2, last], far.at[2, last], sems, 9, y)
    inward[0].wait_recv()
    add_rows(sums.at[0], total.at[me ^ 6], near.at[0], jnp.bfloat16)
    diagonal_x.start()
    diagonal_y.start()
    inward[1].wait_recv()
    add_rows(sums.at[1], total.at[me ^ 2], near.at[1], jnp.bfloat16)
    x_first.start()
    inward[2].wait_recv()
    add_rows(sums.at[2], total.at[me ^ 4], near.at[2], jnp.bfloat16)
    y_last.start()
    diagonal_x.wait_recv()
    add_rows(sums.at[2, first], sums.at[2, first], far.at[0, first], jnp.bfloat16)
    y_first.start()
    diagonal_y.wait_recv()
    add_rows(sums.at[1, last], sums.at[1, last], far.at[0, last], jnp.bfloat16)
    x_last.start()
    inward[3].wait_recv()
    add_rows(out, total.at[me], near.at[3], jnp.float32)
    x_first.wait_recv()
    add_rows(out.at[first], out.at[first], far.at[1, first], jnp.float32)
    y_last.wait_recv()
    add_rows(out.at[last], out.at[last], far.at[2, last], jnp.float32)
    y_first.wait_recv()
    add_rows(out.at[first], out.at[first], far.at[2, first], jnp.float32)
    x_last.wait_recv()
    add_rows(out.at[last], out.at[last], far.at[1, last], jnp.float32)
    for copy in inward + [diagonal_x, diagonal_y, x_first, x_last, y_first, y_last]:
        copy.wait_send()


def plane_scatter(total, ident):
    total = total.astype(jnp.bfloat16)
    if lax.axis_size("ctx") != 8:
        return lax.psum_scatter(total, "ctx", scatter_dimension=0, tiled=True).astype(jnp.float32)
    rows, width = total.shape[0] // 8, total.shape[1]
    return pl.pallas_call(
        scatter_kernel,
        out_shape=jax.ShapeDtypeStruct((rows, width), jnp.float32),
        in_specs=[pl.BlockSpec(memory_space=pltpu.VMEM)],
        out_specs=pl.BlockSpec(memory_space=pltpu.VMEM),
        scratch_shapes=[
            pltpu.VMEM((4, rows, width), jnp.bfloat16),
            pltpu.VMEM((3, rows, width), jnp.bfloat16),
            pltpu.VMEM((3, rows, width), jnp.bfloat16),
            pltpu.SemaphoreType.DMA((10,)),
            pltpu.SemaphoreType.DMA((10,)),
        ],
        compiler_params=pltpu.CompilerParams(collective_id=ident, has_side_effects=True),
        name="plane_scatter",
    )(total.reshape(8, rows, width))


def offloaded_scatter(total):
    return lax.psum_scatter(
        total.astype(jnp.bfloat16), "fsdp", scatter_dimension=0, tiled=True
    ).astype(jnp.float32)


def gains_kernel(size, parts, out, lined, planed, kept, line_send, line_recv, plane_send, plane_recv):
    me, z = lax.axis_index("ctx"), lax.axis_index("fsdp")
    line = [(me, lax.rem(z + i, size)) for i in range(1, size)]
    plane = [(lax.rem(me + i, 8), z) for i in range(1, 8)]
    greet(line + plane)
    first = [
        send(parts.at[peer[1]], lined.at[i], (line_send, line_recv), i, peer) for i, peer in enumerate(line)
    ]
    for copy in first:
        copy.start()
    for copy in first:
        copy.wait_recv()
    kept[...] = parts[z] + sum(lined[i] for i in range(size - 1))
    second = [send(kept, planed.at[i], (plane_send, plane_recv), i, peer) for i, peer in enumerate(plane)]
    for copy in second:
        copy.start()
    for copy in second:
        copy.wait_recv()
    out[...] = kept[...] + sum(planed[i] for i in range(7))
    for copy in first + second:
        copy.wait_send()


def gains_summed(gains, ident):
    size, place = lax.axis_size("fsdp"), lax.axis_index("fsdp")
    share = gains.shape[1] // size
    if lax.axis_size("ctx") != 8:
        whole = lax.psum(gains, ("ctx", "fsdp"))
        return lax.dynamic_slice_in_dim(whole, place * share, share, 1)
    return pl.pallas_call(
        lambda *refs: gains_kernel(size, *refs),
        out_shape=jax.ShapeDtypeStruct((2, share), jnp.float32),
        in_specs=[pl.BlockSpec(memory_space=pltpu.VMEM)],
        out_specs=pl.BlockSpec(memory_space=pltpu.VMEM),
        scratch_shapes=[
            pltpu.VMEM((size - 1, 2, share), jnp.float32),
            pltpu.VMEM((7, 2, share), jnp.float32),
            pltpu.VMEM((2, share), jnp.float32),
            pltpu.SemaphoreType.DMA((size - 1,)),
            pltpu.SemaphoreType.DMA((size - 1,)),
            pltpu.SemaphoreType.DMA((7,)),
            pltpu.SemaphoreType.DMA((7,)),
        ],
        compiler_params=pltpu.CompilerParams(collective_id=ident, has_side_effects=True),
        name="gains_summed",
    )(gains.reshape(2, size, share).transpose(1, 0, 2))


def together(*values):
    return lax.optimization_barrier(values)


def whole_layer(
    tokens,
    block_order,
    w_query,
    w_key,
    w_value,
    w_out,
    w_gate,
    w_up,
    w_down,
    norm_attn,
    norm_mlp,
    cotangent,
):
    inputs = tokens[0].astype(jnp.float32)
    tok_rows, model_width = inputs.shape
    head_size = HD
    scaling = head_size ** (-0.5)
    layout = block_order[0]
    ctx_size = lax.axis_size("ctx")
    ctx_place = lax.axis_index("ctx")
    seq_rows = tok_rows * ctx_size
    block_rows = seq_rows // layout.shape[0]
    own_heads = HEADS // ctx_size
    share = model_width // ctx_size
    positions = slot_positions(layout, jnp.arange(seq_rows, dtype=jnp.int32), block_rows)
    cosine, sine = rotation_tables(positions, head_size)

    out_part = lax.dynamic_slice_in_dim(w_out, (ctx_place * share) % w_out.shape[0], share, 0)
    seq_tokens, grad_b, w_query, w_key, w_value, gains, out_rows = first_gather(
        [tokens[0], cotangent[0]],
        [own_columns(w, ctx_place, ctx_size) for w in (w_query, w_key, w_value)] + [jnp.stack([norm_attn, norm_mlp])],
        out_part,
        0,
    )
    w_query, w_key, w_value = (w.reshape(model_width, share) for w in (w_query, w_key, w_value))
    if out_rows is None:
        out_cols = rows_gathered(own_columns(w_out, ctx_place, ctx_size))
        out_rows = lax.all_to_all(out_cols, "ctx", split_axis=0, concat_axis=1, tiled=True)
    gains = gains.transpose(1, 0, 2).reshape(2, model_width).astype(jnp.float32)
    gain_attn, gain_mlp = gains[0], gains[1]
    ff_share = w_gate.shape[1] // ctx_size
    ff_half = ff_share // 2
    ff_parts = [
        [
            lax.dynamic_slice_in_dim(w, ctx_place * ff_share + half * ff_half, ff_half, 1)
            for w in (w_gate, w_up, w_down)
        ]
        for half in range(2)
    ]
    ff_first, seq_tokens = together(jnp.concatenate(ff_parts[0], axis=1), seq_tokens)
    ff_first = rows_gathered(ff_first)

    scale_attn = rms_scale(inputs)
    normed_attn = inputs * scale_attn
    seq_inputs = seq_tokens.astype(jnp.float32)
    hidden_attn = (seq_inputs * rms_scale(seq_inputs) * gain_attn[None, :]).astype(jnp.bfloat16)
    query, keyed, valued = (
        jnp.dot(hidden_attn, w, preferred_element_type=jnp.float32).reshape(seq_rows, own_heads, head_size)
        for w in (w_query, w_key, w_value)
    )
    query_rot = rotate(query, cosine, sine).astype(jnp.bfloat16)
    key_rot = rotate(keyed, cosine, sine).astype(jnp.bfloat16)
    value_b = valued.astype(jnp.bfloat16)
    allowed = (positions[None, :] <= positions[:, None])[None]
    scores = jnp.einsum("qhd,khd->hqk", query_rot, key_rot, preferred_element_type=jnp.float32) * scaling
    maxima = jnp.max(jnp.where(allowed, scores, neg_large), axis=-1)
    probs = jnp.where(allowed, jnp.exp(scores - maxima[..., None]), 0.0)
    totals = jnp.sum(probs, axis=-1)
    mixed = jnp.einsum("hqk,khd->qhd", probs.astype(jnp.bfloat16), value_b, preferred_element_type=jnp.float32)
    attn_rows = (mixed / totals.T[:, :, None]).astype(jnp.bfloat16).reshape(seq_rows, share)
    log_totals = maxima + jnp.log(totals)

    mid_stream = inputs + plane_scatter(jnp.dot(attn_rows, out_rows, preferred_element_type=jnp.float32), 1)
    scale_mlp = rms_scale(mid_stream)
    normed_mlp = mid_stream * scale_mlp
    (hidden_mlp,) = plane_gather([(normed_mlp * gain_mlp[None, :]).astype(jnp.bfloat16)], 2)
    acted, grad_gate_pre, grad_up_pre = [], [], []
    ff_whole = [jnp.split(ff_first, 3, axis=1)]
    for half in range(2):
        gate_cols, up_cols, down_cols = ff_whole[half]
        gate_pre = jnp.dot(hidden_mlp, gate_cols, preferred_element_type=jnp.float32)
        up_pre = jnp.dot(hidden_mlp, up_cols, preferred_element_type=jnp.float32)
        grad_act = jnp.dot(grad_b, down_cols, preferred_element_type=jnp.float32)
        sigmoid_gate = jax.nn.sigmoid(gate_pre)
        silu_gate = gate_pre * sigmoid_gate
        acted.append((silu_gate * up_pre).astype(jnp.bfloat16))
        grad_gate_pre.append(
            (grad_act * up_pre * sigmoid_gate * (1.0 + gate_pre * (1.0 - sigmoid_gate))).astype(jnp.bfloat16)
        )
        grad_up_pre.append((grad_act * silu_gate).astype(jnp.bfloat16))
        if half == 0:
            parts = [
                contract_rows(grad_b, acted[0]).astype(jnp.bfloat16),
                contract_rows(hidden_mlp, grad_gate_pre[0]).astype(jnp.bfloat16),
                contract_rows(hidden_mlp, grad_up_pre[0]).astype(jnp.bfloat16),
            ]
            second, first_grads = swap(ff_parts[1], parts, 7)
            ff_whole.append(second)
        else:
            parts = [
                contract_rows(grad_b, acted[1]).astype(jnp.bfloat16),
                contract_rows(
                    hidden_mlp, jnp.concatenate([grad_gate_pre[1], grad_up_pre[1]], axis=1)
                ).astype(jnp.bfloat16),
            ]
    parts[0], parts[1], grad_gate_pre[1], grad_up_pre[1], acted[1] = together(
        parts[0], parts[1], grad_gate_pre[1], grad_up_pre[1], acted[1]
    )
    second_grads = [offloaded_scatter(parts[0]), offloaded_scatter(parts[1])]
    grad_down = jnp.concatenate([first_grads[0], second_grads[0]], axis=1)
    grad_gate = jnp.concatenate([first_grads[1], second_grads[1][:, :ff_half]], axis=1)
    grad_up = jnp.concatenate([first_grads[2], second_grads[1][:, ff_half:]], axis=1)
    columns = plane_scatter(
        sum(
            contract_last(grad_gate_pre[half], ff_whole[half][0]) + contract_last(grad_up_pre[half], ff_whole[half][1])
            for half in range(2)
        ),
        4,
    )
    gain_grad_mlp = jnp.sum(columns * normed_mlp, axis=0)
    grad_mid = cotangent[0].astype(jnp.float32) + norm_back(
        columns * gain_mlp[None, :], normed_mlp, scale_mlp
    )
    (grad_mid_b,) = plane_gather([grad_mid.astype(jnp.bfloat16)], 5)
    attn_all = lax.all_gather(attn_rows, "ctx", axis=1, tiled=True)
    part_out = contract_rows(attn_all, own_columns(grad_mid_b, ctx_place, ctx_size)).astype(jnp.bfloat16)
    part_out, grad_mid_b = together(part_out, grad_mid_b)
    grad_out = offloaded_scatter(part_out)
    grad_attn = contract_last(grad_mid_b, out_rows).astype(jnp.bfloat16)
    delta = jnp.sum(
        (grad_attn.astype(jnp.float32) * attn_rows.astype(jnp.float32)).reshape(
            seq_rows, own_heads, head_size
        ),
        axis=-1,
    ).T
    grad_heads = grad_attn.reshape(seq_rows, own_heads, head_size)
    probs = jnp.where(allowed, jnp.exp(scores - log_totals[..., None]), 0.0)
    grad_v = jnp.einsum("hqk,qhd->khd", probs.astype(jnp.bfloat16), grad_heads, preferred_element_type=jnp.float32)
    grad_probs = jnp.einsum("qhd,khd->hqk", grad_heads, value_b, preferred_element_type=jnp.float32)
    grad_scores = (probs * (grad_probs - delta[..., None]) * scaling).astype(jnp.bfloat16)
    grad_q = jnp.einsum("hqk,khd->qhd", grad_scores, key_rot, preferred_element_type=jnp.float32)
    grad_k = jnp.einsum("hqk,qhd->khd", grad_scores, query_rot, preferred_element_type=jnp.float32)
    grad_q, grad_k, grad_v = (
        grad.astype(jnp.bfloat16).reshape(seq_rows, share)
        for grad in (rotate_back(grad_q, cosine, sine), rotate_back(grad_k, cosine, sine), grad_v)
    )
    part_qkv = contract_rows(hidden_attn, jnp.concatenate([grad_q, grad_k, grad_v], axis=1)).astype(jnp.bfloat16)
    part_qkv, grad_q, grad_k, grad_v = together(part_qkv, grad_q, grad_k, grad_v)
    grads_qkv = offloaded_scatter(part_qkv)
    columns = plane_scatter(
        contract_last(grad_q, w_query) + contract_last(grad_k, w_key) + contract_last(grad_v, w_value), 6
    )
    summed = sum(contract_last(acted[half], ff_whole[half][2]) for half in range(2)).astype(jnp.bfloat16)
    summed, columns = together(summed, columns)
    result = mid_stream + plane_scatter(summed, 3)
    gain_grad_attn = jnp.sum(columns * normed_attn, axis=0)
    grad_input = grad_mid + norm_back(columns * gain_attn[None, :], normed_attn, scale_attn)
    gain_own = gains_summed(jnp.stack([gain_grad_attn, gain_grad_mlp]), 8)
    return (
        result[None],
        grad_input[None],
        grads_qkv[:, :share],
        grads_qkv[:, share : 2 * share],
        grads_qkv[:, 2 * share :],
        grad_out,
        grad_gate,
        grad_up,
        grad_down,
        gain_own[0],
        gain_own[1],
    )


def solution(mesh):
    in_specs = (
        P("fsdp", "ctx", None),
        P("fsdp", None),
        P("fsdp", None),
        P("fsdp", None),
        P("fsdp", None),
        P("fsdp", None),
        P("fsdp", None),
        P("fsdp", None),
        P("fsdp", None),
        P("fsdp"),
        P("fsdp"),
        P("fsdp", "ctx", None),
    )
    out_specs = (
        P("fsdp", "ctx", None),
        P("fsdp", "ctx", None),
        P("fsdp", "ctx"),
        P("fsdp", "ctx"),
        P("fsdp", "ctx"),
        P("fsdp", "ctx"),
        P("fsdp", "ctx"),
        P("fsdp", "ctx"),
        P("fsdp", "ctx"),
        P("fsdp"),
        P("fsdp"),
    )
    return jax.shard_map(whole_layer, mesh=mesh, in_specs=in_specs, out_specs=out_specs, check_vma=False)
```

time: 1200 us -> 736 us (0.61)
  waiting for transfers between devices: 938 us -> 105 us
  Pallas kernels: 0 us -> 396 us
  blocking collectives: 27 us -> 0 us
    reduce_scatter x9 -> x4, waiting for transfers between devices: 484 us -> 84.5 us  [offloaded_scatter(): lax.psum_scatter(total.astype(jnp.bfloat16), 'fsdp', scatter_dimension=0,...]
    pallas_call x0 -> x9, Pallas kernels: none -> 396 us  [the longest x1 143 us: swap(): pl.pallas_call(kernel, out_shape=[jax.ShapeDtypeStruct((size,) + weight.s...]
    all_gather x5 -> x1, waiting for transfers between devices: 276 us -> 20.4 us  [rows_gathered(): return lax.all_gather(part, 'fsdp', axis=0, tiled=True)]
    all_gather x5 -> x1, waiting for transfers between devices: 136 us -> 0.02 us  [whole_layer(): attn_all = lax.all_gather(attn_rows, 'ctx', axis=1, tiled=True)]
    unnamed x21 -> x6, waiting for transfers between devices: 28.6 us -> 0.35 us
    dot_general x5 -> x10, matrix products: 29.3 us -> 49.8 us  [contract_last(): lax.dot_general(left, right, (((1,), (1,)), ((), ())), preferred_element_...]
    all_to_all x1 -> x0, waiting for transfers between devices: 14 us -> none  [on_device(): lax.all_to_all(out_cols, 'ctx', split_axis=0, concat_axis=1, tiled=True)]
    dot_general x11 -> x16, matrix products: 74.8 us -> 60.9 us  [the longest x2 10.7 us: whole_layer(): up_pre = jnp.dot(hidden_mlp, up_cols, preferred_element_type=jnp.float32)]
  transfers between devices with their start and end apart: 21 -> 6, of which waited for: 21 -> 3; matrix products, arithmetic and copies ran while one was open for 12% -> 24% of each run, Pallas kernels for 0% -> 45%
where the time goes in v2:
time: 736 us; the launch traced here: 724 us
  Pallas kernels  396 us (54%)
  matrix products  145 us (20%)
  waiting for transfers between devices  105 us (14%)
  other arithmetic  33.7 us (5%)
  local copies, waits for them, and re-layouts  27.4 us (4%)
  between operations  15.4 us (2%)
    pallas_call x1, Pallas kernels, swap(): pl.pallas_call(kernel, out_shape=[jax.ShapeDtypeStruct((size,) + weight.s...  143 us
    pallas_call x4, Pallas kernels, plane_scatter(): pl.pallas_call(scatter_kernel, out_shape=jax.ShapeDtypeStruct((rows, widt...  121 us
    reduce_scatter x4, waiting for transfers between devices, offloaded_scatter(): lax.psum_scatter(total.astype(jnp.bfloat16), 'fsdp', scatter_dimension=0,...  84.5 us
    pallas_call x1, Pallas kernels, first_gather(): pl.pallas_call(kernel, out_shape=[jax.ShapeDtypeStruct(shape, jnp.bfloat1...  73.2 us
    dot_general x10, matrix products, contract_last(): lax.dot_general(left, right, (((1,), (1,)), ((), ())), preferred_element_...  49.8 us
    pallas_call x2, Pallas kernels, plane_gather(): pl.pallas_call(kernel, out_shape=[jax.ShapeDtypeStruct((8,) + part.shape,...  46.2 us
    dot_general x7, matrix products, contract_rows(): lax.dot_general(left, right, (((0,), (0,)), ((), ())), preferred_element_...  34.8 us
    all_gather x1, waiting for transfers between devices, rows_gathered(): return lax.all_gather(part, 'fsdp', axis=0, tiled=True)  20.4 us
  transfers between devices with their start and end apart: 6, of which 3 were waited for; matrix products, arithmetic and copies ran while one was open for 24% of the time, Pallas kernels for 45%

profile of v2, /device:TPU:0, one launch (start us, length us, event | category | flops | bytes accessed | tf_op | source)
XLA Modules:
  0.0 724.3 jit_solution(16861976972204472069)
XLA Ops:
  19.9 73.2 %first_gather.1 = (bf16[8,128,2048]{2,1,0:T(8,128)(2,1)}, bf16[8,128,2048]{2,1,0:T(8,128)(2,1)}, bf16[4,512,256]{2,1,0:T(8,128)(2,1)}, bf16[4,512,256]{2,1,0:T(8...) custom-call(bf16[128,2048]{1,0:T(8,128)(2,1)} %bitcast.134, ...), custom_call_target="tpu_custom_call" | custom-call | tf_op jit(solution)/shard_map/first_gather/pallas_call | solution.py:449
  125.8 46.2 %plane_scatter.4 = f32[128,2048]{1,0:T(8,128)} custom-call(bf16[8,128,2048]{2,1,0:T(8,128)(2,1)} %bitcast.131), custom_call_target="tpu_custom_call" | custom-call | tf_op jit(solution)/shard_map/plane_scatter/pallas_call | solution.py:567
  174.6 22.6 %plane_gather.2 = bf16[8,128,2048]{2,1,0:T(8,128)(2,1)} custom-call(bf16[128,2048]{1,0:T(8,128)(2,1)} %multiply_convert_fusion.7.refs_0_), custom_call_target="tpu_custom_call" | custom-call | tf_op jit(solution)/shard_map/plane_gather/pallas_call | solution.py:404
  197.2 20.4 %all-gather.3.cloned.1.call-done = bf16[2048,1536]{1,0:T(8,128)(2,1)} async-done(((bf16[512,1536]{1,0:T(8,128)(2,1)}), bf16[2048,1536]{1,0:T(8,128)(2,1)}) %all-gather.3.cloned.1.call-update) | async-done | bytes 6291472 | tf_op jit(solution)/shard_map/all_gather | solution.py:66
  217.6 5.3 fusion.29
  240.8 143.5 %swap.1 = (bf16[4,512,512]{2,1,0:T(8,128)(2,1)}, bf16[4,512,512]{2,1,0:T(8,128)(2,1)}, bf16[4,512,512]{2,1,0:T(8,128)(2,1)}, f32[512,512]{1,0:T(8,128)}, f32[512,512]{1,0:T(8,128)}, /*index=5*/f32[512,512]{1,0:T(8,128)}) custom-call(bf16[512,512]{1,0:T(8,128)(2,1)} %get-tuple-element.77.refs_0_, bf16[512,512]{1,0:T(8,128)(2,1)} %get-tuple-element.123.refs_1_, ...), custom_call_target="tpu_custom_call" | custom-call | tf_op jit(solution)/shard_map/swap/pallas_call | solution.py:491
  384.3 5.3 fusion.95
  392.5 4.6 multiply_convert_fusion.2
  401.8 9.6 %convolution_convert_fusion.1 = bf16[2048,1024]{1,0:T(8,128)(2,1)} fusion(bf16[1024,2048]{1,0:T(8,128)(2,1)} %bitcast.150, bf16[1024,512]{1,0:T(8,128)(2,1)} %get-tuple-element.53, bf16[1024,512]{1,0:T(8,128)(2,1)} %get-tuple-element.52), kind=kOutput, calls=%fused_computation.26 | convolution fusion | flops 4301258752 | bytes 10485760 | tf_op jit(solution)/shard_map/dot_general | solution.py:70
  415.8 7.3 %fusion.31 = f32[1024,2048]{1,0:T(8,128)} fusion(bf16[1024,512]{1,0:T(8,128)(2,1)S(1)} %copy-done.43, bf16[2048,1536]{1,0:T(8,128)(2,1)} %all-gather.3.cloned.1.call-done), kind=kOutput, calls=%fused_computation.58 | convolution fusion | flops 2147483648 | bytes 11534336 | tf_op jit(solution)/shard_map/dot_general | solution.py:55
  423.1 7.2 fusion.27
  430.3 11.8 %add_convert_fusion.1 = bf16[1024,2048]{1,0:T(8,128)(2,1)} fusion(f32[1024,2048]{1,0:T(8,128)S(1)} %fusion.97, f32[1024,2048]{1,0:T(8,128)} %fusion.31, f32[1024,2048]{1,0:T(8,128)} %fusion.27, bf16[1024,512]{1,0:T(8,128)(2,1)} %get-tuple-element.53, bf16[2048,512]{1,0:T(8,128)(2,1)} %bitcast.164), kind=kOutput, calls=%fused_computation.13 | convolution fusion | flops 2155872256 | bytes 32505856 | tf_op jit(solution)/shard_map/dot_general | solution.py:55
  442.1 24.7 %plane_scatter.5 = f32[128,2048]{1,0:T(8,128)} custom-call(bf16[8,128,2048]{2,1,0:T(8,128)(2,1)} %bitcast.133), custom_call_target="tpu_custom_call" | custom-call | tf_op jit(solution)/shard_map/plane_scatter/pallas_call | solution.py:567
  470.7 23.6 %plane_gather.3 = bf16[8,128,2048]{2,1,0:T(8,128)(2,1)} custom-call(bf16[128,2048]{1,0:T(8,128)(2,1)} %fusion.84.refs_0_), custom_call_target="tpu_custom_call" | custom-call | tf_op jit(solution)/shard_map/plane_gather/pallas_call | solution.py:404
  494.3 4.6 convolution_convert_fusion.7
  499.0 4.6 bitcast_reduce_fusion
  503.9 9.6 %multiply_convert_fusion = bf16[4,1024,1024]{1,2,0:T(8,128)(2,1)S(1)} fusion(f32[4,1024,1024]{1,2,0:T(8,128)} %copy-done.2, bf16[1024,4,64]{0,2,1:T(8,128)(2,1)} %bitcast.194, bf16[1024,4,64]{0,2,1:T(8,128)(2,1)} %copy-done.44, f32[4,1024]{1,0:T(4,128)S(1)} %bitcast.196, f32[4,1024]{1,0:T(4,128)S(1)} %log_add_fusion, ...), kind=kOutput, calls=%fused_computation | convolution fusion | flops 566231040 | bytes 27295744 | tf_op jit(solution)/shard_map/qhd,khd->hqk/dot_general | solution.py:781
  519.3 8.0 %fusion.46 = bf16[4,64,1024]{2,1,0:T(8,128)(2,1)S(1)} fusion(bf16[1024,4,64]{0,2,1:T(8,128)(2,1)S(1)} %bitcast.195, f32[4,1024,1024]{1,2,0:T(8,128)} %copy-done.2, f32[4,1024]{1,0:T(4,128)S(1)} %log_add_fusion, pred[1024,1024]{0,1:T(8,128)(4,1)S(1)} %broadcast_compare_fusion), kind=kOutput, calls=%fused_computation.77 | convolution fusion | flops 553910272 | bytes 18890752 | tf_op jit(solution)/shard_map/hqk,qhd->khd/dot_general | solution.py:780
  528.1 5.3 convolution_convert_fusion.2
  540.8 25.5 %plane_scatter.6 = f32[128,2048]{1,0:T(8,128)} custom-call(bf16[8,128,2048]{2,1,0:T(8,128)(2,1)} %bitcast.132), custom_call_target="tpu_custom_call" | custom-call | tf_op jit(solution)/shard_map/plane_scatter/pallas_call | solution.py:567
  574.9 25.0 %plane_scatter.7 = f32[128,2048]{1,0:T(8,128)} custom-call(bf16[8,128,2048]{2,1,0:T(8,128)(2,1)} %bitcast.136), custom_call_target="tpu_custom_call" | custom-call | tf_op jit(solution)/shard_map/plane_scatter/pallas_call | solution.py:567
  602.0 12.0 %gains_summed.1 = f32[2,512]{1,0:T(2,128)} custom-call(f32[4,2,512]{2,1,0:T(2,128)} %maximum_bitcast_fusion.refs_0_), custom_call_target="tpu_custom_call" | custom-call | tf_op jit(solution)/shard_map/gains_summed/pallas_call | solution.py:619
  624.3 8.0 %reduce-scatter.5.cloned.1.call-done = bf16[512,768]{1,0:T(8,128)(2,1)} async-done(((bf16[2048,768]{1,0:T(8,128)(2,1)}), bf16[512,768]{1,0:T(8,128)(2,1)}) %reduce-scatter.5.cloned.1.call-update) | async-done | bytes 786448 | tf_op jit(solution)/shard_map/reduce_scatter | solution.py:585
  634.6 76.5 %reduce-scatter.9.cloned.1.call-done = bf16[512,1024]{1,0:T(8,128)(2,1)} async-done(((bf16[2048,1024]{1,0:T(8,128)(2,1)}), bf16[512,1024]{1,0:T(8,128)(2,1)}) %reduce-scatter.9.cloned.1.call-update) | async-done | bytes 1048592 | tf_op jit(solution)/shard_map/reduce_scatter | solution.py:585
  (176 shorter events, 124.4 us)
Async XLA Ops:
  7.2 5.7 copy-start
  7.2 210.4 %all-gather.3.cloned.1.call-start = ((), (), s32[]{:S(2)}) async-start(), calls=%async_computation.4 | async-start | bytes 7864320 | tf_op jit(solution)/shard_map/all_gather | solution.py:66
  93.2 401.2 %all-gather.5.cloned.1.call-start = ((), (), s32[]{:S(2)}) async-start(), calls=%async_computation.5 | async-start | bytes 4718592 | tf_op jit(solution)/shard_map/all_gather | solution.py:767
  96.3 5.7 copy-start.27
  96.3 5.8 copy-start.22
  98.4 7.3 %copy-start.19 = (f32[1024,64]{0,1:T(8,128)}, f32[1024,64]{0,1:T(8,128)S(1)}, u32[]{:S(2)}) copy-start(f32[1024,64]{0,1:T(8,128)S(1)} %get-tuple-element.124) | copy-start | bytes 786436
  107.7 7.0 copy-start.44
  110.9 6.2 copy-start.2
  121.5 497.1 %reduce-scatter.7.cloned.1.call-start = ((), (), s32[]{:S(2)}) async-start(), calls=%async_computation.7 | async-start | bytes 1310720 | tf_op jit(solution)/shard_map/reduce_scatter | solution.py:585
  125.8 46.3 %copy-start.5 = (bf16[1,128,2048]{2,1,0:T(8,128)(2,1)S(1)}, bf16[1,128,2048]{2,1,0:T(8,128)(2,1)}, u32[]{:S(2)}) copy-start(bf16[1,128,2048]{2,1,0:T(8,128)(2,1)} %param.12) | copy-start | bytes 1572868
  217.6 5.9 copy-start.29
  229.2 7.4 %copy-start.38 = (bf16[1024,512]{1,0:T(8,128)(2,1)}, bf16[1024,512]{1,0:T(8,128)(2,1)S(1)}, u32[]{:S(2)}) copy-start(bf16[1024,512]{1,0:T(8,128)(2,1)S(1)} %get-tuple-element.84) | copy-start | bytes 3145732
  384.2 5.4 copy-start.31
  384.3 5.4 copy-start.32
  415.8 7.3 %copy-start.41 = (bf16[1024,512]{1,0:T(8,128)(2,1)S(1)}, bf16[1024,512]{1,0:T(8,128)(2,1)}, u32[]{:S(2)}) copy-start(bf16[1024,512]{1,0:T(8,128)(2,1)} %copy-done.40) | copy-start | bytes 3145732
  442.1 26.2 %copy-start.8 = (bf16[1,128,2048]{2,1,0:T(8,128)(2,1)S(1)}, bf16[1,128,2048]{2,1,0:T(8,128)(2,1)}, u32[]{:S(2)}) copy-start(bf16[1,128,2048]{2,1,0:T(8,128)(2,1)} %param.23) | copy-start | bytes 1572868
  499.0 121.4 %reduce-scatter.11.cloned.1.call-start = ((), (), s32[]{:S(2)}) async-start(), calls=%async_computation.9 | async-start | bytes 2621440 | tf_op jit(solution)/shard_map/reduce_scatter | solution.py:585
  503.7 128.6 %reduce-scatter.5.cloned.1.call-start = ((), (), s32[]{:S(2)}) async-start(), calls=%async_computation.6 | async-start | bytes 3932160 | tf_op jit(solution)/shard_map/reduce_scatter | solution.py:585
  519.3 8.8 %copy-start.15 = (bf16[8,128,2048]{2,1,0:T(8,128)(2,1)S(1)}, bf16[8,128,2048]{2,1,0:T(8,128)(2,1)}, u32[]{:S(2)}) copy-start(bf16[8,128,2048]{2,1,0:T(8,128)(2,1)} %get-tuple-element.39) | copy-start | bytes 12582916
  533.5 177.7 %reduce-scatter.9.cloned.1.call-start = ((), (), s32[]{:S(2)}) async-start(), calls=%async_computation.8 | async-start | bytes 5242880 | tf_op jit(solution)/shard_map/reduce_scatter | solution.py:585
  540.8 25.5 %copy-start.39 = (bf16[1024,512]{1,0:T(8,128)(2,1)S(1)}, bf16[1024,512]{1,0:T(8,128)(2,1)}, u32[]{:S(2)}) copy-start(bf16[1024,512]{1,0:T(8,128)(2,1)} %copy-done.38) | copy-start | bytes 3145732
  574.9 25.0 %copy-start.4 = (f32[128,2048]{1,0:T(8,128)S(1)}, f32[128,2048]{1,0:T(8,128)}, u32[]{:S(2)}) copy-start(f32[128,2048]{1,0:T(8,128)} %plane_scatter.6) | copy-start | bytes 3145732
  574.9 40.4 %copy-start.3 = (f32[128,2048]{1,0:T(8,128)S(1)}, f32[128,2048]{1,0:T(8,128)}, u32[]{:S(2)}) copy-start(f32[128,2048]{1,0:T(8,128)} %plane_scatter.5) | copy-start | bytes 3145732
  634.6 80.9 %copy-start.23 = (f32[512,512]{1,0:T(8,128)S(1)}, f32[512,512]{1,0:T(8,128)}, u32[]{:S(2)}) copy-start(f32[512,512]{1,0:T(8,128)} %get-tuple-element.62) | copy-start | bytes 3145732
  (27 other events, 75.2 us)
Sparse Core Ops, SparseCore 0:
  93.3 124.3 all-gather.2
  220.1 34.7 all-gather.4
  499.1 26.2 reduce-scatter.6
  528.1 42.1 reduce-scatter.10
  572.4 59.8 reduce-scatter.4
  634.4 76.6 reduce-scatter.8
